TPU v7x, 32 devices: a whole 2x2x4 slice. The times are simulated.
32 devices in a mesh: row: 8 (over z, core), col: 4 (over y, x).
Axes of the slice: x: 2, y: 2, z: 4, core: 2. Of those that a mesh axis runs over, the one named last changes fastest.
Arguments:
- energy: float32 [4, 2048, 2048], P('col', 'row'), may hold values from 0.5 to 8
- damage_old: float32 [4, 2048, 2048], P('col', 'row'), may hold values from 0 to 0.8
- crack_seeds: int32 [4, 2048, 2048], P('col', 'row'), may hold values 0 or 1
- irreversible: int32 [4, 2048, 2048], P('col', 'row'), may hold values 0 or 1
- line_inverses: float32 [8, 256, 256], replicated, may hold values from -0.6 to 2.8
- z_inverse: float32 [4, 4], replicated, may hold values from -0.8 to 1.9
Outputs:
- damage: float32 [4, 2048, 2048], P('col', 'row')
- update_norms: float32 [2], replicated
All inputs are finite; a program needn't handle non-finite values. No bound on the sum of `crack_seeds` or of `irreversible` on one device may be relied on, other than what follows from the above.
Results may differ from a plain program's by a relative error of at most 0.0001.
Values sent between devices are 32-bit elements; how exact they have to be, the bound alone decides.
A program may use at most 128 MiB of HBM per device.

v0:
```python
import functools

import jax
import jax.numpy as jnp
from jax import lax
from jax.experimental import pallas as pl
from jax.experimental.pallas import tpu as pltpu
from jax.sharding import PartitionSpec as P

ITERS = 2


KAPPA = 2.0
STEP = 0.02
COUPLE = 0.5
EPSILON = 1e-06
HIGHEST = lax.Precision.HIGHEST


def second_difference(grid_field, along):
    extent = grid_field.shape[along]
    forward_diff = lax.slice_in_dim(grid_field, 1, extent, axis=along) - lax.slice_in_dim(
        grid_field, 0, extent - 1, axis=along
    )
    zero_shape = list(grid_field.shape)
    zero_shape[along] = 1
    zero_rim = jnp.zeros(zero_shape, grid_field.dtype)
    ahead = jnp.concatenate([forward_diff, zero_rim], axis=along)
    behind = jnp.concatenate([zero_rim, forward_diff], axis=along)
    return ahead - behind


def line_solve(line_rows, inverses):
    block_count, block_cells, _ = inverses.shape
    line_count = line_rows.shape[0]
    blocks = line_rows.reshape(line_count, block_count, block_cells)
    products = jnp.einsum("rkb,kcb->rkc", blocks, inverses, precision=lax.Precision.HIGHEST)
    first_col = inverses[:, :, 0]
    last_col = inverses[:, :, block_cells - 1]
    incoming = [jnp.zeros((line_count,), line_rows.dtype)]
    for block_index in range(block_count - 1):
        incoming.append(
            products[:, block_index, block_cells - 1]
            + COUPLE * incoming[block_index] * inverses[block_index, block_cells - 1, 0]
        )
    inflow = jnp.stack(incoming, axis=1)
    forward = products + COUPLE * inflow[:, :, None] * first_col[None]
    head_terms = [jnp.zeros((line_count,), line_rows.dtype) for block_index in range(block_count)]
    carried = forward[:, block_count - 1, 0]
    for block_index in range(block_count - 2, -1, -1):
        head_terms[block_index] = carried
        carried = (
            forward[:, block_index, 0]
            + COUPLE * carried * inverses[block_index, 0, block_cells - 1]
        )
    outflow = jnp.stack(head_terms, axis=1)
    solved = forward + COUPLE * outflow[:, :, None] * last_col[None]
    return solved.reshape(line_count, block_count * block_cells)


def local_turned(energy, damage_old, crack_seeds, irreversible, line_inverses, z_inverse):
    planes, rows_here, line_length = energy.shape
    row_count = lax.axis_size("row")
    col_count = lax.axis_size("col")
    total_planes = planes * col_count
    cell_count = total_planes * rows_here * row_count * line_length
    seeded = crack_seeds == 1
    damage = jnp.where(seeded, 1.0, damage_old)
    lower_bound = jnp.where(irreversible == 1, damage_old, 0.0)
    own_sums = []
    for sweep_index in range(ITERS):
        local_lap = second_difference(damage, 2)
        partial_value = energy - (1.0 + energy) * damage + KAPPA * local_lap
        moved_part, moved_damage = (
            lax.all_to_all(
                lax.all_to_all(
                    jnp.swapaxes(partial_value, 1, 2),
                    "row",
                    split_axis=1,
                    concat_axis=2,
                    tiled=True,
                ),
                "col",
                split_axis=1,
                concat_axis=0,
                tiled=True,
            ),
            lax.all_to_all(
                lax.all_to_all(
                    jnp.swapaxes(damage, 1, 2), "row", split_axis=1, concat_axis=2, tiled=True
                ),
                "col",
                split_axis=1,
                concat_axis=0,
                tiled=True,
            ),
        )
        lap_rest = second_difference(moved_damage, 2) + second_difference(moved_damage, 0)
        turned = moved_part + KAPPA * lap_rest
        turned_shape = turned.shape
        along_y = line_solve(turned.reshape(-1, turned_shape[2]), line_inverses).reshape(
            turned_shape
        )
        along_z = jnp.einsum("zk,kxy->zxy", z_inverse, along_y, precision=lax.Precision.HIGHEST)
        gathered = lax.all_to_all(
            lax.all_to_all(along_z, "row", split_axis=2, concat_axis=1, tiled=True),
            "col",
            split_axis=0,
            concat_axis=1,
            tiled=True,
        )
        piece_cells = gathered.shape[1] // (row_count * col_count)
        reordered = gathered.reshape(planes, col_count, row_count, piece_cells, rows_here)
        restored = jnp.transpose(reordered, (0, 4, 2, 1, 3)).reshape(planes, rows_here, line_length)
        update = STEP * line_solve(restored.reshape(-1, line_length), line_inverses).reshape(
            restored.shape
        )
        clamped = jnp.minimum(jnp.maximum(damage + update, lower_bound), 1.0)
        renewed = jnp.where(seeded, 1.0, clamped)
        own_sum = jnp.sum((renewed - damage) ** 2)
        own_sums.append(own_sum)
        damage = renewed
    global_sums = lax.psum(jnp.stack(own_sums), ("row", "col"))
    update_norms = jnp.sqrt(global_sums / cell_count + EPSILON) / STEP
    return (damage, update_norms)


def line_kernel(
    shape,
    corners,
    z_inv,
    energy,
    damage_hbm,
    seeds_hbm,
    irreversible_hbm,
    inverses,
    out,
    norms,
    damage_old,
    crack_seeds,
    irreversible,
    start,
    bound,
    ez,
    fz,
    dz,
    mix,
    gx,
    gy,
    gx_high,
    gx_low,
    gy_high,
    gy_low,
    h_in,
    gend,
    ab_x,
    ab_y,
    x_send,
    x_all,
    h_send,
    h_recv,
    y_send,
    y_all,
    s_send,
    s_col,
    s_row_send,
    s_row,
    local_sems,
    move_send,
    move_recv,
    back_send,
    back_recv,
    x_ssem,
    x_rsem,
    h_ssem,
    h_rsem,
    v_ssem,
    v_rsem,
    y_ssem,
    y_rsem,
    sc_ssem,
    sc_rsem,
    sr_ssem,
    sr_rsem,
):
    rows, cols, cells, width, x_blocks, blocks, cell_count = shape
    planes = cols
    last = cells - 1
    row, col = lax.axis_index("row"), lax.axis_index("col")
    ends = 8
    tail = 8 - x_blocks

    def slab(who):
        return pl.ds(pl.multiple_of(who * width, width), width)

    def send(src, dst, ssem, rsem, **where):
        copy = pltpu.make_async_remote_copy(
            src_ref=src, dst_ref=dst, send_sem=ssem, recv_sem=rsem,
            device_id=where, device_id_type=pl.DeviceIdType.MESH,
        )
        copy.start()
        return copy

    def weighted(weights, field, kept):
        total = None
        for n in kept:
            term = weights[:, n : n + 1] * field[n : n + 1]
            total = term if total is None else total + term
        return total

    def split(a):
        high = a.astype(jnp.bfloat16)
        return high, (a - high.astype(jnp.float32)).astype(jnp.bfloat16)

    def dot3(a, b):
        def part(u, v):
            return jnp.dot(u, v, preferred_element_type=jnp.float32)

        return part(a[0], b[0]) + (part(a[0], b[1]) + part(a[1], b[0]))

    def line_ends(field):
        tile_lane = lax.broadcasted_iota(jnp.int32, (cells, 128), 1)
        packed = field[:, :128]
        for j in range(x_blocks):
            head = field[:, j * cells : j * cells + 128]
            end = field[:, (j + 1) * cells - 128 : (j + 1) * cells]
            if j > 0:
                head = pltpu.roll(head, j, 1)
                end = pltpu.roll(end, 128 - j, 1)
            packed = jnp.where(tile_lane == j, head, packed)
            packed = jnp.where(tile_lane == 127 - j, end, packed)
        turned = packed.T
        at = lax.broadcasted_iota(jnp.int32, (8, cells), 0)
        kept = (at < x_blocks) | (at >= 8 - x_blocks)
        return jnp.where(kept, jnp.where(at < x_blocks, turned[:8], turned[120:]), 0.0)

    fetch = [
        pltpu.make_async_copy(inverses.at[col * x_blocks + j], gx.at[j], local_sems.at[j])
        for j in range(x_blocks)
    ]
    fetch.append(pltpu.make_async_copy(inverses.at[row], gy, local_sems.at[x_blocks]))
    pulls = [
        pltpu.make_async_copy(damage_hbm, damage_old, local_sems.at[x_blocks + 1]),
        pltpu.make_async_copy(seeds_hbm, crack_seeds, local_sems.at[x_blocks + 2]),
        pltpu.make_async_copy(irreversible_hbm, irreversible, local_sems.at[x_blocks + 3]),
        pltpu.make_async_copy(energy.at[:, slab(col)], ez.at[col], local_sems.at[x_blocks + 4]),
    ]

    moves = []
    inside = pl.ds(8, cells)

    def move(index, src, landing, part=slice(None)):
        sent = []
        for o in range(1, cols):
            peer = lax.rem(col + o, cols)
            sent.append(
                send(src.at[part, slab(peer)], landing, move_send.at[index, o - 1],
                     move_recv.at[index, o - 1], col=peer)
            )
        moves.append(sent)

    move(0, energy, ez.at[col])
    for copy in pulls + fetch:
        copy.start()
    for copy in pulls:
        copy.wait()

    @pl.loop(0, cells // 16)
    def _(i):
        at = pl.ds(pl.multiple_of(i * 16, 16), 16)
        old = damage_old[at, :]
        seeded = crack_seeds[at, :] == 1
        start[at, :] = jnp.where(seeded, 1.0, old)
        bound[at, :] = jnp.where(seeded, 1.0, jnp.where(irreversible[at, :] == 1, old, 0.0))

    move(1, start, dz.at[0, col, inside, :])
    dz[0, col, inside, :] = start[:, slab(col)]
    fz[col] = bound[:, slab(col)]

    lane = lax.broadcasted_iota(jnp.int32, (8, 128), 1)
    sub = lax.broadcasted_iota(jnp.int32, (8, 128), 0)

    def carries(first, final, own):
        zero = jnp.zeros((8, 128), jnp.float32)
        incoming = [zero]
        for k in range(blocks - 1):
            at_last = jnp.where(lane == final(k), 1.0, 0.0)
            incoming.append(at_last + COUPLE * corners[1, k] * incoming[k])
        head = [
            jnp.where(lane == first(k), 1.0, 0.0) + COUPLE * corners[0, k] * incoming[k]
            for k in range(blocks)
        ]
        carried = head[blocks - 1]
        outgoing = [zero] * blocks
        for k in range(blocks - 2, -1, -1):
            outgoing[k] = carried
            carried = head[k] + COUPLE * corners[2, k] * carried
        picked = zero
        even = lax.rem(sub, 2) == 0
        for k in range(blocks):
            value = jnp.where(even, incoming[k], outgoing[k])
            picked = picked + jnp.where(own == k, COUPLE * value, 0.0)
        return picked

    half = lax.div(sub, 2)
    ab_x[...] = carries(
        lambda k: ends * (k // x_blocks) + k % x_blocks,
        lambda k: ends * (k // x_blocks) + 7 - k % x_blocks,
        jnp.where(half < x_blocks, col * x_blocks + half, -1),
    )
    ab_y[...] = carries(
        lambda k: 2 * planes * k + 2 * half,
        lambda k: 2 * planes * k + 2 * half + 1,
        row + 0 * sub,
    )

    for copy in fetch:
        copy.wait()
    gend[...] = jnp.zeros_like(gend)
    for j in range(x_blocks):
        turned = gx[j].T
        gx_high[j], gx_low[j] = split(turned)
        block = slice(j * cells, (j + 1) * cells)
        gend[2 * j : 2 * j + 1, block] = turned[:1]
        gend[2 * j + 1 : 2 * j + 2, block] = turned[last:]
    gy_high[...], gy_low[...] = split(gy[...])

    wide_row = lax.broadcasted_iota(jnp.int32, (8, width), 0)
    wide_lane = lax.broadcasted_iota(jnp.int32, (8, width), 1)
    has_left, has_right = col > 0, col < cols - 1
    degree_x = (
        2.0
        - jnp.where((wide_lane == 0) & jnp.logical_not(has_left), 1.0, 0.0)
        - jnp.where((wide_lane == width - 1) & jnp.logical_not(has_right), 1.0, 0.0)
    )
    at_first, at_last = wide_lane == 0, wide_lane == width - 1
    upper = jnp.where(row > 0, 1.0, 0.0)
    lower = jnp.where(row < rows - 1, 1.0, 0.0)

    def finish(sent):
        for copy in sent:
            copy.wait()

    def line_rows(z):
        return pl.ds(pl.multiple_of(z * cells, cells), cells)

    finish(moves[1])

    totals = []
    for it in range(ITERS):
        @pl.loop(0, planes)
        def _(z):
            h_send[it, :, line_rows(z)] = line_ends(dz[it, z, inside, :])

        halo = [
            send(h_send.at[it], h_recv.at[it, pl.ds(0, 8), :], h_ssem.at[it, 0], h_rsem.at[it, 0],
                 col=lax.rem(col + 1, cols)),
            send(h_send.at[it], h_recv.at[it, pl.ds(8, 8), :], h_ssem.at[it, 1], h_rsem.at[it, 1],
                 col=lax.rem(col + cols - 1, cols)),
            send(dz.at[it, :, pl.ds(cells, 8), :], dz.at[it, :, pl.ds(0, 8), :], v_ssem.at[it, 0],
                 v_rsem.at[it, 0], row=lax.rem(row + 1, rows)),
            send(dz.at[it, :, pl.ds(8, 8), :], dz.at[it, :, pl.ds(cells + 8, 8), :],
                 v_ssem.at[it, 1], v_rsem.at[it, 1], row=lax.rem(row + rows - 1, rows)),
        ]
        if it == 0:
            finish(moves[0])
            pieces = [slice(0, cells // 2), slice(cells // 2, cells)]
            move(2, bound, fz.at[col, pieces[0], :], pieces[0])
        finish(halo)

        @pl.loop(0, planes)
        def _(z):
            left = h_recv[it, tail : tail + 1, line_rows(z)]
            right = h_recv[it, 8:9, line_rows(z)]
            at = lax.broadcasted_iota(jnp.int32, (128, cells), 0)
            left = jnp.where((at == 0) & has_left, left, 0.0)
            right = jnp.where((at == 127) & has_right, right, 0.0)
            h_in[z] = (left + right).T

        @pl.loop(0, cells // 8)
        def _(i):
            near = pl.ds(pl.multiple_of(i * 8, 8), 24)
            here = pl.ds(pl.multiple_of(i * 8, 8), 8)
            y_at = wide_row + i * 8
            top = jnp.where(y_at == 0, upper, 1.0)
            bottom = jnp.where(y_at == last, lower, 1.0)
            wins = [dz[it, z, near, :] for z in range(planes)]
            mids = [w[8:16] for w in wins]
            residual = []
            for z in range(planes):
                d = mids[z]
                above = pltpu.roll(wins[z], 1, 0)[8:16]
                below = pltpu.roll(wins[z], 23, 0)[8:16]
                lap = top * (above - d) + bottom * (below - d)
                lap = lap + jnp.where(at_first, 0.0, pltpu.roll(d, 1, 1))
                lap = lap + jnp.where(at_last, 0.0, pltpu.roll(d, width - 1, 1))
                edges = h_in[z, here, :]
                lap = lap + jnp.where(at_first, jnp.tile(edges, (1, width // 128)), 0.0)
                lap = lap + jnp.where(at_last, jnp.tile(edges, (1, width // 128)), 0.0)
                lap = lap - degree_x * d
                if z > 0:
                    lap = lap + (mids[z - 1] - d)
                if z < planes - 1:
                    lap = lap + (mids[z + 1] - d)
                e = ez[z, here, :]
                residual.append(e - (1.0 + e) * d + KAPPA * lap)
            for z in range(planes):
                total = z_inv[z, 0] * residual[0]
                for k in range(1, planes):
                    total = total + z_inv[z, k] * residual[k]
                mix[z, here, :] = total

        @pl.loop(0, planes)
        def _(z):
            along = jnp.concatenate(
                [
                    dot3(
                        split(mix[z, :, j * cells : (j + 1) * cells]), (gx_high[j], gx_low[j])
                    )
                    for j in range(x_blocks)
                ],
                axis=1,
            )
            both = dot3((gy_high[...], gy_low[...]), split(along))
            mix[z] = both
            x_send[it, :, line_rows(z)] = line_ends(both)

        swaps = []
        for o in range(1, cols):
            swaps.append(
                send(x_send.at[it], x_all.at[it, pl.ds(pl.multiple_of(col * 8, 8), 8), :],
                     x_ssem.at[it, o - 1], x_rsem.at[it, o - 1], col=lax.rem(col + o, cols))
            )
        x_all[it, pl.ds(pl.multiple_of(col * 8, 8), 8), :] = x_send[it]
        if it == 0:
            move(3, bound, fz.at[col, pieces[1], :], pieces[1])
        finish(swaps)

        for z in range(planes):
            kept = [
                ends * c + n for c in range(cols) for n in range(ends)
                if n < x_blocks or n >= ends - x_blocks
            ]
            carry = weighted(ab_x[...], x_all[it, :, z * cells : (z + 1) * cells], kept)
            carry = jnp.concatenate([carry, jnp.zeros((120, cells), jnp.float32)], axis=0).T
            parts = []
            for j in range(x_blocks):
                block = slice(j * cells, (j + 1) * cells)
                enter = carry[:, 2 * j : 2 * j + 1] * gend[2 * j : 2 * j + 1, block]
                leave = carry[:, 2 * j + 1 : 2 * j + 2] * gend[2 * j + 1 : 2 * j + 2, block]
                parts.append(mix[z, :, block] + enter + leave)
            value = jnp.concatenate(parts, axis=1)
            mix[z] = value
            y_send[it, 2 * z : 2 * z + 1, :] = value[:1]
            y_send[it, 2 * z + 1 : 2 * z + 2, :] = value[last:]

        swaps = []
        own = pl.ds(pl.multiple_of(row * 2 * planes, 2 * planes), 2 * planes)
        for o in range(1, rows):
            swaps.append(
                send(y_send.at[it], y_all.at[it, own, :], y_ssem.at[it, o - 1],
                     y_rsem.at[it, o - 1], row=lax.rem(row + o, rows))
            )
        y_all[it, own, :] = y_send[it]
        finish(swaps)
        if it == 0:
            finish(moves[2] + moves[3])
        carry_y = weighted(ab_y[...], y_all[it], range(rows * 2 * planes))

        squares = jnp.zeros((8, width), jnp.float32)
        for z in range(planes):
            enter, leave = carry_y[2 * z : 2 * z + 1], carry_y[2 * z + 1 : 2 * z + 2]

            def settle(i, acc, z=z, enter=enter, leave=leave):
                here = pl.ds(pl.multiple_of(i * 8, 8), 8)
                padded = pl.ds(pl.multiple_of(i * 8 + 8, 8), 8)
                g_first, g_last = gy[here, 0:1], gy[here, last : last + 1]
                solved = mix[z, here, :] + g_first * enter + g_last * leave
                d = dz[it, z, padded, :]
                renewed = jnp.minimum(jnp.maximum(d + STEP * solved, fz[z, here, :]), 1.0)
                dz[it + 1, z, padded, :] = renewed
                change = renewed - d
                return acc + change * change

            squares = lax.fori_loop(0, cells // 8, settle, squares, unroll=2)
        totals.append(jnp.sum(squares))

    s_send[...] = jnp.where(sub == 0, totals[0], jnp.where(sub == 1, totals[1], 0.0))
    final = dz.at[ITERS]
    shares = []
    for o in range(1, cols):
        shares.append(
            send(s_send, s_col.at[o - 1], sc_ssem.at[o - 1], sc_rsem.at[o - 1],
                 col=lax.rem(col + o, cols))
        )
    backs = []
    for o in range(1, cols):
        peer = lax.rem(col + o, cols)
        backs.append(
            send(final.at[peer, inside, :], out.at[:, slab(col)], back_send.at[o - 1],
                 back_recv.at[o - 1], col=peer)
        )
    out[:, slab(col)] = final[col, inside, :]
    finish(shares)
    total = s_send[...]
    for o in range(1, cols):
        total = total + s_col[o - 1]
    s_row_send[...] = total
    shares = []
    for o in range(1, rows):
        shares.append(
            send(s_row_send, s_row.at[o - 1], sr_ssem.at[o - 1], sr_rsem.at[o - 1],
                 row=lax.rem(row + o, rows))
        )
    finish(shares)
    for o in range(1, rows):
        total = total + s_row[o - 1]
    norms[...] = jnp.sqrt(total / cell_count + EPSILON) / STEP
    finish(backs)


def local(energy, damage_old, crack_seeds, irreversible, line_inverses, z_inverse):
    planes, cells, line_length = energy.shape
    rows, cols = lax.axis_size("row"), lax.axis_size("col")
    blocks, _, _ = line_inverses.shape
    width = line_length // cols
    x_blocks = width // cells
    last = cells - 1
    lines = cols * cells
    shape = (rows, cols, cells, width, x_blocks, blocks, float(cols * rows * cells * line_length))
    corners = jnp.stack(
        [line_inverses[:, 0, 0], line_inverses[:, last, 0], line_inverses[:, 0, last]]
    )
    f32 = jnp.float32
    dma = pltpu.SemaphoreType.DMA
    vmem = pl.BlockSpec(memory_space=pltpu.VMEM)
    smem = pl.BlockSpec(memory_space=pltpu.SMEM)
    damage, norms = pl.pallas_call(
        functools.partial(line_kernel, shape),
        out_shape=(
            jax.ShapeDtypeStruct((cells, line_length), f32),
            jax.ShapeDtypeStruct((8, 128), f32),
        ),
        in_specs=[smem, smem] + [pl.BlockSpec(memory_space=pl.ANY)] * 5,
        out_specs=(vmem, vmem),
        scratch_shapes=[
            pltpu.VMEM((cells, line_length), f32),
            pltpu.VMEM((cells, line_length), jnp.int32),
            pltpu.VMEM((cells, line_length), jnp.int32),
            pltpu.VMEM((cells, line_length), f32),
            pltpu.VMEM((cells, line_length), f32),
            pltpu.VMEM((cols, cells, width), f32),
            pltpu.VMEM((cols, cells, width), f32),
            pltpu.VMEM((ITERS + 1, cols, cells + 16, width), f32),
            pltpu.VMEM((cols, cells, width), f32),
            pltpu.VMEM((x_blocks, cells, cells), f32),
            pltpu.VMEM((cells, cells), f32),
            pltpu.VMEM((x_blocks, cells, cells), jnp.bfloat16),
            pltpu.VMEM((x_blocks, cells, cells), jnp.bfloat16),
            pltpu.VMEM((cells, cells), jnp.bfloat16),
            pltpu.VMEM((cells, cells), jnp.bfloat16),
            pltpu.VMEM((cols, cells, 128), f32),
            pltpu.VMEM((8, width), f32),
            pltpu.VMEM((8, 128), f32),
            pltpu.VMEM((8, 128), f32),
            pltpu.VMEM((ITERS, 8, lines), f32),
            pltpu.VMEM((ITERS, 8 * cols, lines), f32),
            pltpu.VMEM((ITERS, 8, lines), f32),
            pltpu.VMEM((ITERS, 16, lines), f32),
            pltpu.VMEM((ITERS, 2 * cols, width), f32),
            pltpu.VMEM((ITERS, 2 * cols * rows, width), f32),
            pltpu.VMEM((8, 128), f32),
            pltpu.VMEM((cols - 1, 8, 128), f32),
            pltpu.VMEM((8, 128), f32),
            pltpu.VMEM((rows - 1, 8, 128), f32),
            dma((x_blocks + 5,)),
            dma((4, cols - 1)),
            dma((4, cols - 1)),
            dma((cols - 1,)),
            dma((cols - 1,)),
            dma((ITERS, cols - 1)),
            dma((ITERS, cols - 1)),
            dma((ITERS, 2)),
            dma((ITERS, 2)),
            dma((ITERS, 2)),
            dma((ITERS, 2)),
            dma((ITERS, rows - 1)),
            dma((ITERS, rows - 1)),
            dma((cols - 1,)),
            dma((cols - 1,)),
            dma((rows - 1,)),
            dma((rows - 1,)),
        ],
        compiler_params=pltpu.CompilerParams(
            has_side_effects=True, vmem_limit_bytes=60 * 1024 * 1024
        ),
        name="line_iterations",
    )(
        corners,
        z_inverse,
        energy[0],
        damage_old[0],
        crack_seeds[0],
        irreversible[0],
        line_inverses,
    )
    return damage[None], norms[:ITERS, 0]


def solution(mesh):
    def local_any(energy, damage_old, crack_seeds, irreversible, line_inverses, z_inverse):
        rows, cols = mesh.shape["row"], mesh.shape["col"]
        block_cells = line_inverses.shape[1]
        width = energy.shape[2] // cols
        whole_blocks = (
            energy.shape[0] == 1
            and energy.shape[1] == block_cells
            and width % block_cells == 0
            and 2 * (width // block_cells) <= 8
            and 2 * cols == 8
            and 8 * max(rows, cols) <= 128
            and min(rows, cols) > 2
        )
        chosen = local if whole_blocks else local_turned
        return chosen(energy, damage_old, crack_seeds, irreversible, line_inverses, z_inverse)

    return jax.shard_map(
        local_any,
        mesh=mesh,
        in_specs=(
            P("col", "row", None),
            P("col", "row", None),
            P("col", "row", None),
            P("col", "row", None),
            P(),
            P(),
        ),
        out_specs=(P("col", "row", None), P()),
        check_vma=False,
    )
```

profile of v0, /device:TPU:0, one launch (start us, length us, event | category | flops | bytes accessed | tf_op | source)
XLA Modules:
  0.0 152.4 jit_solution(13866483624588286445)
XLA Ops:
  0.6 1.0 slice_reduce_fusion.2
  1.6 0.6 pad_maximum_fusion.corners
  2.2 145.7 %line_iterations.1 = (f32[256,2048]{1,0:T(8,128)}, f32[8,128]{1,0:T(8,128)}) custom-call(f32[3,8]{1,0:T(4,128)} %pad_maximum_fusion.corners, f32[4,4]{1,0:T(4,128)} %z_inv.1, f32[256,2048]{1,0:T(8,128)} %bitcast.8, f32[256,2048]{1,0:T(8,128)} %bitcast.9, s32[256,2048]{1,0:T(8,128)} %bitcast.10, s32[256,2048]{1,0:T(8,128)} %bitcast.11, f32[8,256,256]{2,1,0:T(8,128)} %inverses.1), custom_call_target="tpu_custom_call" | custom-call | tf_op jit(solution)/shard_map/line_iterations/pallas_call | solution.py:538
  148.0 1.3 slice_reduce_fusion.3
  149.3 3.1 %copy.9 = f32[1,256,2048]{2,1,0:T(8,128)} copy(f32[1,256,2048]{2,1,0:T(8,128)} %bitcast.12) | data formatting | bytes 4194304
where the time goes:
time: 153 us; the launch traced here: 152 us
  Pallas kernels  146 us (95%)
  local copies, waits for them, and re-layouts  5.44 us (4%)
    pallas_call x1, Pallas kernels, local(): pl.pallas_call(functools.partial(line_kernel, shape), out_shape=(jax.Shap...  146 us
    unnamed x1, local copies, waits for them, and re-layouts  3.13 us

commit v1 on v0

v1 whole, which is shorter than its diff:
```python
import functools

import jax
import jax.numpy as jnp
from jax import lax
from jax.experimental import pallas as pl
from jax.experimental.pallas import tpu as pltpu
from jax.sharding import PartitionSpec as P

ITERS = 2


KAPPA = 2.0
STEP = 0.02
COUPLE = 0.5
EPSILON = 1e-06
HIGHEST = lax.Precision.HIGHEST


def second_difference(grid_field, along):
    extent = grid_field.shape[along]
    forward_diff = lax.slice_in_dim(grid_field, 1, extent, axis=along) - lax.slice_in_dim(
        grid_field, 0, extent - 1, axis=along
    )
    zero_shape = list(grid_field.shape)
    zero_shape[along] = 1
    zero_rim = jnp.zeros(zero_shape, grid_field.dtype)
    ahead = jnp.concatenate([forward_diff, zero_rim], axis=along)
    behind = jnp.concatenate([zero_rim, forward_diff], axis=along)
    return ahead - behind


def line_solve(line_rows, inverses):
    block_count, block_cells, _ = inverses.shape
    line_count = line_rows.shape[0]
    blocks = line_rows.reshape(line_count, block_count, block_cells)
    products = jnp.einsum("rkb,kcb->rkc", blocks, inverses, precision=lax.Precision.HIGHEST)
    first_col = inverses[:, :, 0]
    last_col = inverses[:, :, block_cells - 1]
    incoming = [jnp.zeros((line_count,), line_rows.dtype)]
    for block_index in range(block_count - 1):
        incoming.append(
            products[:, block_index, block_cells - 1]
            + COUPLE * incoming[block_index] * inverses[block_index, block_cells - 1, 0]
        )
    inflow = jnp.stack(incoming, axis=1)
    forward = products + COUPLE * inflow[:, :, None] * first_col[None]
    head_terms = [jnp.zeros((line_count,), line_rows.dtype) for block_index in range(block_count)]
    carried = forward[:, block_count - 1, 0]
    for block_index in range(block_count - 2, -1, -1):
        head_terms[block_index] = carried
        carried = (
            forward[:, block_index, 0]
            + COUPLE * carried * inverses[block_index, 0, block_cells - 1]
        )
    outflow = jnp.stack(head_terms, axis=1)
    solved = forward + COUPLE * outflow[:, :, None] * last_col[None]
    return solved.reshape(line_count, block_count * block_cells)


def local_turned(energy, damage_old, crack_seeds, irreversible, line_inverses, z_inverse):
    planes, rows_here, line_length = energy.shape
    row_count = lax.axis_size("row")
    col_count = lax.axis_size("col")
    total_planes = planes * col_count
    cell_count = total_planes * rows_here * row_count * line_length
    seeded = crack_seeds == 1
    damage = jnp.where(seeded, 1.0, damage_old)
    lower_bound = jnp.where(irreversible == 1, damage_old, 0.0)
    own_sums = []
    for sweep_index in range(ITERS):
        local_lap = second_difference(damage, 2)
        partial_value = energy - (1.0 + energy) * damage + KAPPA * local_lap
        moved_part, moved_damage = (
            lax.all_to_all(
                lax.all_to_all(
                    jnp.swapaxes(partial_value, 1, 2),
                    "row",
                    split_axis=1,
                    concat_axis=2,
                    tiled=True,
                ),
                "col",
                split_axis=1,
                concat_axis=0,
                tiled=True,
            ),
            lax.all_to_all(
                lax.all_to_all(
                    jnp.swapaxes(damage, 1, 2), "row", split_axis=1, concat_axis=2, tiled=True
                ),
                "col",
                split_axis=1,
                concat_axis=0,
                tiled=True,
            ),
        )
        lap_rest = second_difference(moved_damage, 2) + second_difference(moved_damage, 0)
        turned = moved_part + KAPPA * lap_rest
        turned_shape = turned.shape
        along_y = line_solve(turned.reshape(-1, turned_shape[2]), line_inverses).reshape(
            turned_shape
        )
        along_z = jnp.einsum("zk,kxy->zxy", z_inverse, along_y, precision=lax.Precision.HIGHEST)
        gathered = lax.all_to_all(
            lax.all_to_all(along_z, "row", split_axis=2, concat_axis=1, tiled=True),
            "col",
            split_axis=0,
            concat_axis=1,
            tiled=True,
        )
        piece_cells = gathered.shape[1] // (row_count * col_count)
        reordered = gathered.reshape(planes, col_count, row_count, piece_cells, rows_here)
        restored = jnp.transpose(reordered, (0, 4, 2, 1, 3)).reshape(planes, rows_here, line_length)
        update = STEP * line_solve(restored.reshape(-1, line_length), line_inverses).reshape(
            restored.shape
        )
        clamped = jnp.minimum(jnp.maximum(damage + update, lower_bound), 1.0)
        renewed = jnp.where(seeded, 1.0, clamped)
        own_sum = jnp.sum((renewed - damage) ** 2)
        own_sums.append(own_sum)
        damage = renewed
    global_sums = lax.psum(jnp.stack(own_sums), ("row", "col"))
    update_norms = jnp.sqrt(global_sums / cell_count + EPSILON) / STEP
    return (damage, update_norms)


def line_kernel(
    shape,
    z_inv,
    energy,
    damage_hbm,
    seeds_hbm,
    irreversible_hbm,
    inverses,
    out,
    norms,
    damage_old,
    crack_seeds,
    irreversible,
    start,
    bound,
    ez,
    fz,
    landing,
    dz,
    final,
    w_high,
    w_low,
    mix,
    corner,
    gx,
    gy,
    gx_high,
    gx_low,
    gy_high,
    gy_low,
    gy_ends,
    gend,
    ab_x,
    ab_y,
    carry_rows,
    x_send,
    x_all,
    y_send,
    y_all,
    s_send,
    s_row,
    s_col_send,
    s_col,
    local_sems,
    e_ssem,
    e_rsem,
    d_ssem,
    d_rsem,
    f_ssem,
    f_rsem,
    back_ssem,
    back_rsem,
    x_ssem,
    x_rsem,
    v_ssem,
    v_rsem,
    y_ssem,
    y_rsem,
    sc_ssem,
    sc_rsem,
    sr_ssem,
    sr_rsem,
):
    rows, cols, cells, width, x_blocks, blocks, cell_count = shape
    planes = cols
    last = cells - 1
    groups = width // 128
    pieces = 4
    piece = cells // pieces
    ends = 8
    f32 = jnp.float32
    row, col = lax.axis_index("row"), lax.axis_index("col")
    row_peers = [lax.rem(row + o, rows) for o in range(1, rows)]
    col_peers = [lax.rem(col + o, cols) for o in range(1, cols)]

    def slab(who):
        return pl.ds(pl.multiple_of(who * width, width), width)

    def eight(at):
        return pl.ds(pl.multiple_of(at, 8), 8)

    def send(src, dst, ssem, rsem, **where):
        copy = pltpu.make_async_remote_copy(
            src_ref=src, dst_ref=dst, send_sem=ssem, recv_sem=rsem,
            device_id=where, device_id_type=pl.DeviceIdType.MESH,
        )
        copy.start()
        return copy

    def finish(sent):
        for copy in sent:
            copy.wait()

    def weighted(weights, field, kept):
        total = None
        for n in kept:
            term = weights[:, n : n + 1] * field[n : n + 1]
            total = term if total is None else total + term
        return total

    def split(a):
        high = a.astype(jnp.bfloat16)
        return high, (a - high.astype(f32)).astype(jnp.bfloat16)

    def dot3(a, b):
        def part(u, v):
            return jnp.dot(u, v, preferred_element_type=f32)

        return part(a[0], b[0]) + (part(a[0], b[1]) + part(a[1], b[0]))

    def line_ends(field):
        tile_lane = lax.broadcasted_iota(jnp.int32, (cells, 128), 1)
        packed = field[:, :128]
        for j in range(x_blocks):
            begin = field[:, j * cells : j * cells + 128]
            end = field[:, (j + 1) * cells - 128 : (j + 1) * cells]
            if j > 0:
                begin = pltpu.roll(begin, j, 1)
                end = pltpu.roll(end, 128 - j, 1)
            packed = jnp.where(tile_lane == j, begin, packed)
            packed = jnp.where(tile_lane == 127 - j, end, packed)
        turned = packed.T
        at = lax.broadcasted_iota(jnp.int32, (8, cells), 0)
        return jnp.where(at < x_blocks, turned[:8], turned[120:])

    barrier = pltpu.get_barrier_semaphore()
    for peer in col_peers:
        pl.semaphore_signal(
            barrier, inc=1, device_id={"col": peer}, device_id_type=pl.DeviceIdType.MESH
        )
    for peer in row_peers:
        pl.semaphore_signal(
            barrier, inc=1, device_id={"row": peer}, device_id_type=pl.DeviceIdType.MESH
        )

    pulls = [
        pltpu.make_async_copy(damage_hbm, damage_old, local_sems.at[0]),
        pltpu.make_async_copy(seeds_hbm, crack_seeds, local_sems.at[1]),
        pltpu.make_async_copy(irreversible_hbm, irreversible, local_sems.at[2]),
    ]
    fetch = [
        pltpu.make_async_copy(energy.at[:, slab(col)], ez.at[col], local_sems.at[3]),
        pltpu.make_async_copy(inverses.at[row], gy, local_sems.at[4]),
    ]
    for n in range(4):
        down, over = (cells - 8) * (n // 2), (cells - 128) * (n % 2)
        fetch.append(
            pltpu.make_async_copy(
                inverses.at[:, pl.ds(down, 8), pl.ds(over, 128)], corner.at[n], local_sems.at[5 + n]
            )
        )
    for j in range(x_blocks):
        fetch.append(
            pltpu.make_async_copy(inverses.at[col * x_blocks + j], gx.at[j], local_sems.at[9 + j])
        )
    for copy in pulls + fetch:
        copy.start()
    pl.semaphore_wait(barrier, rows + cols - 2)

    def move(src, landing_at, ssem, rsem):
        return [
            send(src.at[:, slab(peer)], landing_at, ssem.at[n], rsem.at[n], col=peer)
            for n, peer in enumerate(col_peers)
        ]

    def move_bound(index):
        at = pl.ds(index * piece, piece)
        return [
            send(bound.at[at, slab(peer)], fz.at[col, at, :], f_ssem.at[index, n],
                 f_rsem.at[index, n], col=peer)
            for n, peer in enumerate(col_peers)
        ]

    moved_e = move(energy, ez.at[col], e_ssem, e_rsem)
    finish(pulls)

    @pl.loop(0, cells // 16)
    def _(i):
        at = pl.ds(pl.multiple_of(i * 16, 16), 16)
        old = damage_old[at, :]
        seeded = crack_seeds[at, :] == 1
        start[at, :] = jnp.where(seeded, 1.0, old)
        bound[at, :] = jnp.where(seeded, 1.0, jnp.where(irreversible[at, :] == 1, old, 0.0))

    moved_d = move(start, landing.at[col], d_ssem, d_rsem)
    moved_f = {n: move_bound(n) for n in (0, pieces - 1)}
    landing[col] = start[:, slab(col)]
    fz[col] = bound[:, slab(col)]

    lane = lax.broadcasted_iota(jnp.int32, (8, 128), 1)
    sub = lax.broadcasted_iota(jnp.int32, (8, 128), 0)
    finish(fetch)

    def corner_of(down, over, k):
        tile = corner[2 * down + over, k]
        at = (7 if down else 0, 127 if over else 0)
        return jnp.broadcast_to(tile[at[0] : at[0] + 1, at[1] : at[1] + 1], (8, 128))

    def hot(index):
        return jnp.where(lane == index, 1.0, 0.0)

    def carries(first, final_of, own, lower=None, upper=None):
        zero = jnp.zeros((8, 128), f32)
        firsts, finals = [], []
        for k in range(blocks):
            begin, end = hot(first(k)), hot(final_of(k))
            low = None if lower is None else lower(k)
            high = None if upper is None else upper(k)
            if low is not None:
                begin = begin + corner_of(0, 0, k) * hot(low)
                end = end + corner_of(1, 0, k) * hot(low)
            if high is not None:
                begin = begin + corner_of(0, 1, k) * hot(high)
                end = end + corner_of(1, 1, k) * hot(high)
            firsts.append(begin)
            finals.append(end)
        incoming = [zero]
        for k in range(blocks - 1):
            incoming.append(finals[k] + COUPLE * corner_of(1, 0, k) * incoming[k])
        heads = [
            firsts[k] + COUPLE * corner_of(0, 0, k) * incoming[k] for k in range(blocks)
        ]
        carried = heads[blocks - 1]
        outgoing = [zero] * blocks
        for k in range(blocks - 2, -1, -1):
            outgoing[k] = carried
            carried = heads[k] + COUPLE * corner_of(0, 1, k) * carried
        picked = zero
        even = lax.rem(sub, 2) == 0
        for k in range(blocks):
            enter, leave = COUPLE * incoming[k], COUPLE * outgoing[k]
            if lower is not None and lower(k) is not None:
                enter = enter + hot(lower(k))
            if upper is not None and upper(k) is not None:
                leave = leave + hot(upper(k))
            picked = picked + jnp.where(own == k, jnp.where(even, enter, leave), 0.0)
        return picked

    half = lax.div(sub, 2)

    def left_of(k):
        c = k // x_blocks
        return ends * (c - 1) + x_blocks + 1 if k % x_blocks == 0 and c > 0 else None

    def right_of(k):
        c = k // x_blocks
        return ends * (c + 1) + x_blocks if k % x_blocks == x_blocks - 1 and c < cols - 1 else None

    ab_x[...] = carries(
        lambda k: ends * (k // x_blocks) + k % x_blocks,
        lambda k: ends * (k // x_blocks) + 7 - k % x_blocks,
        jnp.where(half < x_blocks, col * x_blocks + half, -1),
        left_of,
        right_of,
    )
    ab_y[...] = carries(
        lambda k: 2 * planes * k + 2 * half,
        lambda k: 2 * planes * k + 2 * half + 1,
        row + 0 * sub,
    )

    for j in range(x_blocks):
        turned = gx[j].T
        gx_high[j], gx_low[j] = split(turned)
        gend[2 * j] = jnp.broadcast_to(turned[:1], (8, cells))
        gend[2 * j + 1] = jnp.broadcast_to(turned[last:], (8, cells))
    gy_high[...], gy_low[...] = split(gy[...])
    gy_ends[0] = jnp.broadcast_to(gy[:, :1], (cells, 128))
    gy_ends[1] = jnp.broadcast_to(gy[:, last:], (cells, 128))

    first_col = jnp.where(col == 0, 1.0, 0.0)
    last_col = jnp.where(col == cols - 1, 1.0, 0.0)
    lane16 = lax.broadcasted_iota(jnp.int32, (16, 128), 1)
    at_first, at_last = lane16 == 0, lane16 == 127

    finish(moved_d)

    @pl.loop(0, cells // 8)
    def _(i):
        for z in range(planes):
            tile = landing[z, eight(i * 8), :]
            for g in range(groups):
                dz[0, z, g, eight(i * 8 + 8), :] = tile[:, g * 128 : (g + 1) * 128]

    def share_rows(it):
        return [
            send(dz.at[it, :, :, pl.ds(cells, 8), :], dz.at[it, :, :, pl.ds(0, 8), :],
                 v_ssem.at[it, 0], v_rsem.at[it, 0], row=lax.rem(row + 1, rows)),
            send(dz.at[it, :, :, pl.ds(8, 8), :], dz.at[it, :, :, pl.ds(cells + 8, 8), :],
                 v_ssem.at[it, 1], v_rsem.at[it, 1], row=lax.rem(row + rows - 1, rows)),
        ]

    def mirror(it):
        for z in range(planes):
            for g in range(groups):
                dz[it, z, g, 7:8, :] = jnp.where(
                    row == 0, dz[it, z, g, 8:9, :], dz[it, z, g, 7:8, :]
                )
                dz[it, z, g, cells + 8 : cells + 9, :] = jnp.where(
                    row == rows - 1,
                    dz[it, z, g, cells + 7 : cells + 8, :],
                    dz[it, z, g, cells + 8 : cells + 9, :],
                )

    def residual(it, low, high):
        @pl.loop(low // 16, high // 16)
        def _(i):
            base = pl.multiple_of(i * 16, 16)
            here = pl.ds(base, 16)
            padded = pl.ds(pl.multiple_of(base + 8, 8), 16)
            for g in range(groups):
                lanes = slice(g * 128, (g + 1) * 128)
                mids = [dz[it, z, g, padded, :] for z in range(planes)]
                value = []
                for z in range(planes):
                    d = mids[z]
                    near = dz[it, z, g, pl.ds(base + 7, 16), :] + dz[it, z, g, pl.ds(base + 9, 16), :]
                    before = d * first_col
                    if g > 0:
                        before = pltpu.roll(dz[it, z, g - 1, padded, :], 1, 1)
                    after = d * last_col
                    if g < groups - 1:
                        after = pltpu.roll(dz[it, z, g + 1, padded, :], 127, 1)
                    near = near + jnp.where(at_first, before, pltpu.roll(d, 1, 1))
                    near = near + jnp.where(at_last, after, pltpu.roll(d, 127, 1))
                    sides = 4
                    if z > 0:
                        near = near + mids[z - 1]
                        sides += 1
                    if z < planes - 1:
                        near = near + mids[z + 1]
                        sides += 1
                    e = ez[z, here, lanes]
                    value.append((e - (e + (1.0 + KAPPA * sides)) * d) + KAPPA * near)
                for z in range(planes):
                    total = z_inv[z, 0] * value[0]
                    for k in range(1, planes):
                        total = total + z_inv[z, k] * value[k]
                    w_high[z, here, lanes], w_low[z, here, lanes] = split(total)

    def products(it):
        @pl.loop(0, planes)
        def _(z):
            along = jnp.concatenate(
                [
                    dot3(
                        (w_high[z, :, j * cells : (j + 1) * cells],
                         w_low[z, :, j * cells : (j + 1) * cells]),
                        (gx_high[j], gx_low[j]),
                    )
                    for j in range(x_blocks)
                ],
                axis=1,
            )
            both = dot3((gy_high[...], gy_low[...]), split(along))
            mix[z] = both
            x_send[it, :, pl.ds(pl.multiple_of(z * cells, cells), cells)] = line_ends(both)

    def edges(it):
        tile_lane = lax.broadcasted_iota(jnp.int32, (cells, 128), 1)
        packed = jnp.zeros((cells, 128), f32)
        for z in range(planes):
            begin = dz[it, z, 0, pl.ds(8, cells), :]
            end = dz[it, z, groups - 1, pl.ds(8, cells), :]
            if z > 0:
                begin = pltpu.roll(begin, z, 1)
            end = pltpu.roll(end, planes + z + 1, 1)
            packed = jnp.where(tile_lane == z, begin, packed)
            packed = jnp.where(tile_lane == planes + z, end, packed)
        turned = dot3((gy_high[...], gy_low[...]), split(packed)).T
        for z in range(planes):
            for side in range(2):
                total = None
                for k in range(planes):
                    n = side * planes + k
                    term = (KAPPA * z_inv[z, k]) * turned[n : n + 1]
                    total = term if total is None else total + term
                x_send[it, x_blocks + side : x_blocks + side + 1,
                       z * cells : (z + 1) * cells] = total

    kept_x = [
        ends * c + n for c in range(cols) for n in range(ends)
        if n < x_blocks + 2 or n >= ends - x_blocks
    ]

    def x_share(it):
        own = pl.ds(pl.multiple_of(col * ends, ends), ends)
        sent = [
            send(x_send.at[it], x_all.at[it, own, :], x_ssem.at[it, n], x_rsem.at[it, n], col=peer)
            for n, peer in enumerate(col_peers)
        ]
        x_all[it, own, :] = x_send[it]
        return sent

    def y_share(it):
        lines = []
        for z in range(planes):
            lines.append(weighted(ab_x[...], x_all[it, :, z * cells : (z + 1) * cells], kept_x))
        for z in range(planes):
            for top, at in ((0, 0), (1, last)):
                for j in range(x_blocks):
                    block = slice(j * cells, (j + 1) * cells)
                    line = (
                        mix[z, at : at + 1, block]
                        + lines[z][2 * j : 2 * j + 1, at : at + 1] * gend[2 * j, :1, :]
                        + lines[z][2 * j + 1 : 2 * j + 2, at : at + 1] * gend[2 * j + 1, :1, :]
                    )
                    y_send[it, 2 * z + top : 2 * z + top + 1, block] = line
        own = pl.ds(pl.multiple_of(row * 2 * planes, 2 * planes), 2 * planes)
        sent = [
            send(y_send.at[it], y_all.at[it, own, :], y_ssem.at[it, n], y_rsem.at[it, n], row=peer)
            for n, peer in enumerate(row_peers)
        ]
        y_all[it, own, :] = y_send[it]
        stacked = jnp.concatenate(
            lines + [jnp.zeros((128 - 8 * planes, cells), f32)], axis=0
        ).T
        for t in range(cells // 8):
            here = slice(t * 8, t * 8 + 8)
            tile = stacked[here]
            for z in range(planes):
                for j in range(x_blocks):
                    block = slice(j * cells, (j + 1) * cells)
                    n = 8 * z + 2 * j
                    mix[z, here, block] = (
                        mix[z, here, block]
                        + tile[:, n : n + 1] * gend[2 * j]
                        + tile[:, n + 1 : n + 2] * gend[2 * j + 1]
                    )
        finish(sent)
        carry = weighted(ab_y[...], y_all[it], range(rows * 2 * planes))
        for n in range(2 * planes):
            carry_rows[n] = jnp.broadcast_to(carry[n : n + 1], (8, width))

    def settle(it, low, high, squares):
        def step(i, acc):
            here, padded = eight(i * 8), eight(i * 8 + 8)
            g_first = jnp.concatenate([gy_ends[0, here, :]] * groups, axis=1)
            g_last = jnp.concatenate([gy_ends[1, here, :]] * groups, axis=1)
            for z in range(planes):
                solved = mix[z, here, :] + g_first * carry_rows[2 * z] + g_last * carry_rows[2 * z + 1]
                d = jnp.concatenate([dz[it, z, g, padded, :] for g in range(groups)], axis=1)
                renewed = jnp.minimum(jnp.maximum(d + STEP * solved, fz[z, here, :]), 1.0)
                if it + 1 < ITERS:
                    for g in range(groups):
                        dz[it + 1, z, g, padded, :] = renewed[:, g * 128 : (g + 1) * 128]
                else:
                    final[z, here, :] = renewed
                change = renewed - d
                acc = acc + change * change
            return acc

        return lax.fori_loop(low // 8, high // 8, step, squares)

    totals = []
    blank = jnp.zeros((8, width), f32)

    shared = share_rows(0)
    finish(moved_e)
    finish(shared)
    mirror(0)
    residual(0, 0, cells)
    products(0)
    edges(0)
    sent = x_share(0)
    for n in range(1, pieces - 1):
        moved_f[n] = move_bound(n)
    finish(sent)
    y_share(0)

    squares = blank
    finish(moved_f[0])
    squares = settle(0, 0, piece, squares)
    finish(moved_f[pieces - 1])
    squares = settle(0, cells - piece, cells, squares)
    shared = share_rows(1)
    residual(1, cells - piece + 16, cells - 16)
    for n in range(1, pieces - 1):
        finish(moved_f[n])
        squares = settle(0, n * piece, (n + 1) * piece, squares)
        low = 16 if n == 1 else n * piece - 16
        high = (n + 1) * piece - 16
        residual(1, low, high if n < pieces - 2 else high + 32)
    totals.append(jnp.sum(squares))
    finish(shared)
    mirror(1)
    residual(1, 0, 16)
    residual(1, cells - 16, cells)
    products(1)
    edges(1)
    finish(x_share(1))
    y_share(1)

    def give_back(n):
        at = pl.ds(n * piece, piece)
        return [
            send(final.at[peer, at, :], out.at[at, slab(col)], back_ssem.at[n, m],
                 back_rsem.at[n, m], col=peer)
            for m, peer in enumerate(col_peers)
        ]

    squares = blank
    backs = []
    for n in range(pieces):
        squares = settle(ITERS - 1, n * piece, (n + 1) * piece, squares)
        if n < 2:
            backs += give_back(n)
    totals.append(jnp.sum(squares))
    s_send[...] = jnp.where(sub == 0, totals[0], jnp.where(sub == 1, totals[1], 0.0))
    shares = [
        send(s_send, s_row.at[n], sr_ssem.at[n], sr_rsem.at[n], row=peer)
        for n, peer in enumerate(row_peers)
    ]
    out[:, slab(col)] = final[col]
    finish(shares)
    total = s_send[...]
    for n in range(rows - 1):
        total = total + s_row[n]
    s_col_send[...] = total
    shares = [
        send(s_col_send, s_col.at[n], sc_ssem.at[n], sc_rsem.at[n], col=peer)
        for n, peer in enumerate(col_peers)
    ]
    for n in range(2, pieces):
        backs += give_back(n)
    finish(shares)
    for n in range(cols - 1):
        total = total + s_col[n]
    norms[...] = jnp.sqrt(total / cell_count + EPSILON) / STEP
    finish(backs)


def local(energy, damage_old, crack_seeds, irreversible, line_inverses, z_inverse):
    planes, cells, line_length = energy.shape
    rows, cols = lax.axis_size("row"), lax.axis_size("col")
    blocks, _, _ = line_inverses.shape
    width = line_length // cols
    x_blocks = width // cells
    lines = cols * cells
    pieces = 4
    shape = (rows, cols, cells, width, x_blocks, blocks, float(cols * rows * cells * line_length))
    f32 = jnp.float32
    bf16 = jnp.bfloat16
    dma = pltpu.SemaphoreType.DMA
    vmem = pl.BlockSpec(memory_space=pltpu.VMEM)
    smem = pl.BlockSpec(memory_space=pltpu.SMEM)
    damage, norms = pl.pallas_call(
        functools.partial(line_kernel, shape),
        out_shape=(
            jax.ShapeDtypeStruct((cells, line_length), f32),
            jax.ShapeDtypeStruct((8, 128), f32),
        ),
        in_specs=[smem] + [pl.BlockSpec(memory_space=pl.ANY)] * 5,
        out_specs=(vmem, vmem),
        scratch_shapes=[
            pltpu.VMEM((cells, line_length), f32),
            pltpu.VMEM((cells, line_length), jnp.int32),
            pltpu.VMEM((cells, line_length), jnp.int32),
            pltpu.VMEM((cells, line_length), f32),
            pltpu.VMEM((cells, line_length), f32),
            pltpu.VMEM((cols, cells, width), f32),
            pltpu.VMEM((cols, cells, width), f32),
            pltpu.VMEM((cols, cells, width), f32),
            pltpu.VMEM((ITERS, cols, width // 128, cells + 16, 128), f32),
            pltpu.VMEM((cols, cells, width), f32),
            pltpu.VMEM((cols, cells, width), bf16),
            pltpu.VMEM((cols, cells, width), bf16),
            pltpu.VMEM((cols, cells, width), f32),
            pltpu.VMEM((4, blocks, 8, 128), f32),
            pltpu.VMEM((x_blocks, cells, cells), f32),
            pltpu.VMEM((cells, cells), f32),
            pltpu.VMEM((x_blocks, cells, cells), bf16),
            pltpu.VMEM((x_blocks, cells, cells), bf16),
            pltpu.VMEM((cells, cells), bf16),
            pltpu.VMEM((cells, cells), bf16),
            pltpu.VMEM((2, cells, 128), f32),
            pltpu.VMEM((2 * x_blocks, 8, cells), f32),
            pltpu.VMEM((8, 128), f32),
            pltpu.VMEM((8, 128), f32),
            pltpu.VMEM((2 * cols, 8, width), f32),
            pltpu.VMEM((ITERS, 8, lines), f32),
            pltpu.VMEM((ITERS, 8 * cols, lines), f32),
            pltpu.VMEM((ITERS, 2 * cols, width), f32),
            pltpu.VMEM((ITERS, 2 * cols * rows, width), f32),
            pltpu.VMEM((8, 128), f32),
            pltpu.VMEM((rows - 1, 8, 128), f32),
            pltpu.VMEM((8, 128), f32),
            pltpu.VMEM((cols - 1, 8, 128), f32),
            dma((x_blocks + 9,)),
            dma((cols - 1,)),
            dma((cols - 1,)),
            dma((cols - 1,)),
            dma((cols - 1,)),
            dma((pieces, cols - 1)),
            dma((pieces, cols - 1)),
            dma((pieces, cols - 1)),
            dma((pieces, cols - 1)),
            dma((ITERS, cols - 1)),
            dma((ITERS, cols - 1)),
            dma((ITERS, 2)),
            dma((ITERS, 2)),
            dma((ITERS, rows - 1)),
            dma((ITERS, rows - 1)),
            dma((cols - 1,)),
            dma((cols - 1,)),
            dma((rows - 1,)),
            dma((rows - 1,)),
        ],
        compiler_params=pltpu.CompilerParams(
            has_side_effects=True, collective_id=0, vmem_limit_bytes=60 * 1024 * 1024
        ),
        name="line_iterations",
    )(
        z_inverse,
        energy[0],
        damage_old[0],
        crack_seeds[0],
        irreversible[0],
        line_inverses,
    )
    return damage[None], norms[:ITERS, 0]


def solution(mesh):
    def local_any(energy, damage_old, crack_seeds, irreversible, line_inverses, z_inverse):
        rows, cols = mesh.shape["row"], mesh.shape["col"]
        block_cells = line_inverses.shape[1]
        width = energy.shape[2] // cols
        whole_blocks = (
            energy.shape[0] == 1
            and energy.shape[1] == block_cells
            and width % block_cells == 0
            and 2 * (width // block_cells) + 2 <= 8
            and block_cells % 128 == 0
            and 2 * cols == 8
            and 8 * max(rows, cols) <= 128
            and min(rows, cols) > 2
        )
        chosen = local if whole_blocks else local_turned
        return chosen(energy, damage_old, crack_seeds, irreversible, line_inverses, z_inverse)

    return jax.shard_map(
        local_any,
        mesh=mesh,
        in_specs=(
            P("col", "row", None),
            P("col", "row", None),
            P("col", "row", None),
            P("col", "row", None),
            P(),
            P(),
        ),
        out_specs=(P("col", "row", None), P()),
        check_vma=False,
    )
```

time: 153 us -> 126 us (0.82)
  Pallas kernels: 146 us -> 121 us
    pallas_call x1, Pallas kernels: 146 us -> 121 us  [local(): pl.pallas_call(functools.partial(line_kernel, shape), out_shape=(jax.Shap...]
where the time goes in v1:
time: 126 us
  Pallas kernels  121 us (96%)
  local copies, waits for them, and re-layouts  4.45 us (4%)
    pallas_call x1, Pallas kernels, local(): pl.pallas_call(functools.partial(line_kernel, shape), out_shape=(jax.Shap...  121 us
    unnamed x1, local copies, waits for them, and re-layouts  3.13 us

profile of v1, /device:TPU:0, one launch (start us, length us, event | category | flops | bytes accessed | tf_op | source)
XLA Modules:
  0.0 125.9 jit_solution(3907886188005435627)
XLA Ops:
  0.6 120.8 %line_iterations.1 = (f32[256,2048]{1,0:T(8,128)}, f32[8,128]{1,0:T(8,128)}) custom-call(f32[4,4]{1,0:T(4,128)} %z_inv.1, f32[256,2048]{1,0:T(8,128)} %bitcast.6, f32[256,2048]{1,0:T(8,128)} %bitcast.7, s32[256,2048]{1,0:T(8,128)} %bitcast.8, s32[256,2048]{1,0:T(8,128)} %bitcast.9, f32[8,256,256]{2,1,0:T(8,128)} %inverses.1), custom_call_target="tpu_custom_call" | custom-call | tf_op jit(solution)/shard_map/line_iterations/pallas_call | solution.py:674
  121.4 1.3 %slice_reduce_fusion = f32[2]{0:T(128)} fusion(f32[8,128]{1,0:T(8,128)} %get-tuple-element.5), kind=kLoop, calls=%fused_computation | loop fusion | bytes 16 | tf_op jit(solution)/shard_map/slice | solution.py:748
  122.8 3.1 %copy.9 = f32[1,256,2048]{2,1,0:T(8,128)} copy(f32[1,256,2048]{2,1,0:T(8,128)} %bitcast.5) | data formatting | bytes 4194304

commit v2 on v1

--- a/solution.py
+++ b/solution.py
@@ -147,19 +147,25 @@
     final,
     w_high,
     w_low,
+    a_high,
+    a_low,
     mix,
     corner,
     gx,
     gy,
     gx_high,
     gx_low,
-    gy_high,
-    gy_low,
+    gy_both,
     gy_ends,
     gend,
-    ab_x,
-    ab_y,
+    wx_send,
+    wx_in,
+    wx_own,
+    wy_in,
+    wy_turn,
     carry_rows,
+    own_rows,
+    y_base,
     x_send,
     x_all,
     y_send,
@@ -188,13 +194,11 @@
     sr_ssem,
     sr_rsem,
 ):
-    rows, cols, cells, width, x_blocks, blocks, cell_count = shape
+    rows, cols, cells, width, x_blocks, blocks, cell_count, cuts, backs_at = shape
     planes = cols
     last = cells - 1
     groups = width // 128
-    pieces = 4
-    piece = cells // pieces
-    ends = 8
+    kinds = 2 * x_blocks + 2
     f32 = jnp.float32
     row, col = lax.axis_index("row"), lax.axis_index("col")
     row_peers = [lax.rem(row + o, rows) for o in range(1, rows)]
@@ -218,22 +222,12 @@
         for copy in sent:
             copy.wait()
 
-    def weighted(weights, field, kept):
-        total = None
-        for n in kept:
-            term = weights[:, n : n + 1] * field[n : n + 1]
-            total = term if total is None else total + term
-        return total
-
     def split(a):
         high = a.astype(jnp.bfloat16)
         return high, (a - high.astype(f32)).astype(jnp.bfloat16)
 
-    def dot3(a, b):
-        def part(u, v):
-            return jnp.dot(u, v, preferred_element_type=f32)
-
-        return part(a[0], b[0]) + (part(a[0], b[1]) + part(a[1], b[0]))
+    def dot(a, b):
+        return jnp.dot(a, b, preferred_element_type=f32)
 
     def line_ends(field):
         tile_lane = lax.broadcasted_iota(jnp.int32, (cells, 128), 1)
@@ -243,12 +237,10 @@
             end = field[:, (j + 1) * cells - 128 : (j + 1) * cells]
             if j > 0:
                 begin = pltpu.roll(begin, j, 1)
-                end = pltpu.roll(end, 128 - j, 1)
-            packed = jnp.where(tile_lane == j, begin, packed)
-            packed = jnp.where(tile_lane == 127 - j, end, packed)
-        turned = packed.T
-        at = lax.broadcasted_iota(jnp.int32, (8, cells), 0)
-        return jnp.where(at < x_blocks, turned[:8], turned[120:])
+                packed = jnp.where(tile_lane == j, begin, packed)
+            end = pltpu.roll(end, x_blocks + j + 1, 1)
+            packed = jnp.where(tile_lane == x_blocks + j, end, packed)
+        return packed.T[:8]
 
     barrier = pltpu.get_barrier_semaphore()
     for peer in col_peers:
@@ -284,21 +276,18 @@
         copy.start()
     pl.semaphore_wait(barrier, rows + cols - 2)
 
-    def move(src, landing_at, ssem, rsem):
+    def move_piece(src, target, index, ssem, rsem):
+        at = pl.ds(cuts[index], cuts[index + 1] - cuts[index])
         return [
-            send(src.at[:, slab(peer)], landing_at, ssem.at[n], rsem.at[n], col=peer)
+            send(src.at[at, slab(peer)], target.at[col, at, :], ssem.at[index, n],
+                 rsem.at[index, n], col=peer)
             for n, peer in enumerate(col_peers)
         ]
 
-    def move_bound(index):
-        at = pl.ds(index * piece, piece)
-        return [
-            send(bound.at[at, slab(peer)], fz.at[col, at, :], f_ssem.at[index, n],
-                 f_rsem.at[index, n], col=peer)
-            for n, peer in enumerate(col_peers)
-        ]
-
-    moved_e = move(energy, ez.at[col], e_ssem, e_rsem)
+    moved_e = [
+        send(energy.at[:, slab(peer)], ez.at[col], e_ssem.at[n], e_rsem.at[n], col=peer)
+        for n, peer in enumerate(col_peers)
+    ]
     finish(pulls)
 
     @pl.loop(0, cells // 16)
@@ -309,14 +298,20 @@
         start[at, :] = jnp.where(seeded, 1.0, old)
         bound[at, :] = jnp.where(seeded, 1.0, jnp.where(irreversible[at, :] == 1, old, 0.0))
 
-    moved_d = move(start, landing.at[col], d_ssem, d_rsem)
-    moved_f = {n: move_bound(n) for n in (0, pieces - 1)}
+    order = (0, 3, 1, 2)
+    moved_d = {n: move_piece(start, landing, n, d_ssem, d_rsem) for n in order}
+    moved_f = {n: move_piece(bound, fz, n, f_ssem, f_rsem) for n in order[:2]}
     landing[col] = start[:, slab(col)]
     fz[col] = bound[:, slab(col)]
 
     lane = lax.broadcasted_iota(jnp.int32, (8, 128), 1)
     sub = lax.broadcasted_iota(jnp.int32, (8, 128), 0)
+    upper_half = sub < planes
+    zero = jnp.zeros((8, 128), f32)
     finish(fetch)
+
+    def lane_of(a, n):
+        return jnp.broadcast_to(a[:, n : n + 1], (8, 128))
 
     def corner_of(down, over, k):
         tile = corner[2 * down + over, k]
@@ -326,19 +321,18 @@
     def hot(index):
         return jnp.where(lane == index, 1.0, 0.0)
 
-    def carries(first, final_of, own, lower=None, upper=None):
-        zero = jnp.zeros((8, 128), f32)
+    def carries(first, final_of, lower=None, upper=None):
         firsts, finals = [], []
+        low = [None if lower is None else lower(k) for k in range(blocks)]
+        high = [None if upper is None else upper(k) for k in range(blocks)]
         for k in range(blocks):
             begin, end = hot(first(k)), hot(final_of(k))
-            low = None if lower is None else lower(k)
-            high = None if upper is None else upper(k)
-            if low is not None:
-                begin = begin + corner_of(0, 0, k) * hot(low)
-                end = end + corner_of(1, 0, k) * hot(low)
-            if high is not None:
-                begin = begin + corner_of(0, 1, k) * hot(high)
-                end = end + corner_of(1, 1, k) * hot(high)
+            if low[k] is not None:
+                begin = begin + corner_of(0, 0, k) * hot(low[k])
+                end = end + corner_of(1, 0, k) * hot(low[k])
+            if high[k] is not None:
+                begin = begin + corner_of(0, 1, k) * hot(high[k])
+                end = end + corner_of(1, 1, k) * hot(high[k])
             firsts.append(begin)
             finals.append(end)
         incoming = [zero]
@@ -352,46 +346,78 @@
         for k in range(blocks - 2, -1, -1):
             outgoing[k] = carried
             carried = heads[k] + COUPLE * corner_of(0, 1, k) * carried
-        picked = zero
-        even = lax.rem(sub, 2) == 0
+        enter, leave = [], []
         for k in range(blocks):
-            enter, leave = COUPLE * incoming[k], COUPLE * outgoing[k]
-            if lower is not None and lower(k) is not None:
-                enter = enter + hot(lower(k))
-            if upper is not None and upper(k) is not None:
-                leave = leave + hot(upper(k))
-            picked = picked + jnp.where(own == k, jnp.where(even, enter, leave), 0.0)
-        return picked
-
-    half = lax.div(sub, 2)
+            enter.append(COUPLE * incoming[k] + (zero if low[k] is None else hot(low[k])))
+            leave.append(COUPLE * outgoing[k] + (zero if high[k] is None else hot(high[k])))
+        return incoming, outgoing, enter, leave
+
+    def picked(which, options):
+        total = zero
+        for n, option in enumerate(options):
+            if option is not None:
+                total = total + jnp.where(which == n, option, 0.0)
+        return total
+
+    def at_own(c, weights):
+        return pltpu.roll(weights, 128 - 8 * c, 1) if c > 0 else weights
 
     def left_of(k):
         c = k // x_blocks
-        return ends * (c - 1) + x_blocks + 1 if k % x_blocks == 0 and c > 0 else None
+        return 8 * (c - 1) + 2 * x_blocks + 1 if k % x_blocks == 0 and c > 0 else None
 
     def right_of(k):
         c = k // x_blocks
-        return ends * (c + 1) + x_blocks if k % x_blocks == x_blocks - 1 and c < cols - 1 else None
-
-    ab_x[...] = carries(
-        lambda k: ends * (k // x_blocks) + k % x_blocks,
-        lambda k: ends * (k // x_blocks) + 7 - k % x_blocks,
-        jnp.where(half < x_blocks, col * x_blocks + half, -1),
+        return 8 * (c + 1) + 2 * x_blocks if k % x_blocks == x_blocks - 1 and c < cols - 1 else None
+
+    incoming, outgoing, enter, leave = carries(
+        lambda k: 8 * (k // x_blocks) + k % x_blocks,
+        lambda k: 8 * (k // x_blocks) + x_blocks + k % x_blocks,
         left_of,
         right_of,
     )
-    ab_y[...] = carries(
-        lambda k: 2 * planes * k + 2 * half,
-        lambda k: 2 * planes * k + 2 * half + 1,
-        row + 0 * sub,
+    to_right = picked(col, [
+        at_own(c, incoming[(c + 1) * x_blocks] + hot(8 * c + 2 * x_blocks + 1) / COUPLE)
+        if c < cols - 1 else None
+        for c in range(cols)
+    ])
+    to_left = picked(col, [
+        at_own(c, leave[c * x_blocks - 1] / COUPLE) if c > 0 else None for c in range(cols)
+    ])
+    for n in range(kinds):
+        wx_send[n] = jnp.where(upper_half, lane_of(to_right, n), lane_of(to_left, n))
+    for m in range(2 * x_blocks):
+        table = (enter, leave)[m % 2]
+        everywhere = picked(col, [table[c * x_blocks + m // 2] for c in range(cols)])
+        here = picked(col, [at_own(c, table[c * x_blocks + m // 2]) for c in range(cols)])
+        for c in range(cols):
+            from_left = jnp.where(col > c, lane_of(everywhere, 8 * c + 2 * x_blocks - 1), 0.0)
+            from_right = jnp.where(col < c, lane_of(everywhere, 8 * c), 0.0)
+            wx_in[m, c] = jnp.where(upper_half, from_left, from_right)
+        for n in range(kinds):
+            wx_own[m, n] = lane_of(here, n)
+
+    incoming, outgoing, enter, leave = carries(lambda k: 2 * k, lambda k: 2 * k + 1)
+    enters, leaves = picked(row, enter), picked(row, leave)
+    for k in range(rows):
+        wy_in[0, k] = lane_of(enters, 2 * k + 1)
+        wy_in[1, k] = jnp.where(row >= k, lane_of(leaves, 2 * k + 1), lane_of(leaves, 2 * k))
+    wy_turn[...] = picked(
+        row, [lane_of(outgoing[k - 1], 2 * k + 1) if k > 0 else None for k in range(rows)]
     )
 
+    upper_wide = lax.broadcasted_iota(jnp.int32, (8, cells), 0) < planes
     for j in range(x_blocks):
         turned = gx[j].T
         gx_high[j], gx_low[j] = split(turned)
-        gend[2 * j] = jnp.broadcast_to(turned[:1], (8, cells))
-        gend[2 * j + 1] = jnp.broadcast_to(turned[last:], (8, cells))
-    gy_high[...], gy_low[...] = split(gy[...])
+        for side, at in ((0, 0), (1, last)):
+            line = jnp.broadcast_to(turned[at : at + 1], (8, cells))
+            gend[side, j] = line
+            if j == 0:
+                gend[side, x_blocks] = line
+            else:
+                gend[side, x_blocks] = jnp.where(upper_wide, gend[side, x_blocks], line)
+    gy_both[:cells], gy_both[cells:] = split(gy[...])
     gy_ends[0] = jnp.broadcast_to(gy[:, :1], (cells, 128))
     gy_ends[1] = jnp.broadcast_to(gy[:, last:], (cells, 128))
 
@@ -400,14 +426,13 @@
     lane16 = lax.broadcasted_iota(jnp.int32, (16, 128), 1)
     at_first, at_last = lane16 == 0, lane16 == 127
 
-    finish(moved_d)
-
-    @pl.loop(0, cells // 8)
-    def _(i):
-        for z in range(planes):
-            tile = landing[z, eight(i * 8), :]
-            for g in range(groups):
-                dz[0, z, g, eight(i * 8 + 8), :] = tile[:, g * 128 : (g + 1) * 128]
+    def regroup(low, high):
+        @pl.loop(low // 8, high // 8)
+        def _(i):
+            for z in range(planes):
+                tile = landing[z, eight(i * 8), :]
+                for g in range(groups):
+                    dz[0, z, g, eight(i * 8 + 8), :] = tile[:, g * 128 : (g + 1) * 128]
 
     def share_rows(it):
         return [
@@ -465,23 +490,36 @@
                         total = total + z_inv[z, k] * value[k]
                     w_high[z, here, lanes], w_low[z, here, lanes] = split(total)
 
-    def products(it):
-        @pl.loop(0, planes)
-        def _(z):
-            along = jnp.concatenate(
-                [
-                    dot3(
-                        (w_high[z, :, j * cells : (j + 1) * cells],
-                         w_low[z, :, j * cells : (j + 1) * cells]),
-                        (gx_high[j], gx_low[j]),
-                    )
-                    for j in range(x_blocks)
-                ],
-                axis=1,
-            )
-            both = dot3((gy_high[...], gy_low[...]), split(along))
+    def x_product(ranges):
+        for j in range(x_blocks):
+            block = slice(j * cells, (j + 1) * cells)
+            parts = [(z, low, high) for z in range(planes) for low, high in ranges]
+            high_rows = jnp.concatenate([w_high[z, a:b, block] for z, a, b in parts], axis=0)
+            low_rows = jnp.concatenate([w_low[z, a:b, block] for z, a, b in parts], axis=0)
+            count = high_rows.shape[0]
+            twice = dot(jnp.concatenate([high_rows, low_rows], axis=0), gx_high[j])
+            along = twice[:count] + (twice[count:] + dot(high_rows, gx_low[j]))
+            at = 0
+            for z, a, b in parts:
+                a_high[z, a:b, block], a_low[z, a:b, block] = split(along[at : at + b - a])
+                at += b - a
+
+    def y_times(high, low):
+        twice = dot(gy_both[...], high)
+        return twice[:cells] + (twice[cells:] + dot(gy_both[:cells], low))
+
+    def y_product():
+        for z in range(planes):
+            both = y_times(a_high[z], a_low[z])
             mix[z] = both
-            x_send[it, :, pl.ds(pl.multiple_of(z * cells, cells), cells)] = line_ends(both)
+            turned = line_ends(both)
+            for n in range(2 * x_blocks):
+                own_rows[n, z : z + 1, :] = turned[n : n + 1]
+                own_rows[n, planes + z : planes + z + 1, :] = turned[n : n + 1]
+            for side, at in ((0, 0), (1, last)):
+                for j in range(x_blocks):
+                    n = j * planes + z
+                    y_base[side, n : n + 1, :] = both[at : at + 1, j * cells : (j + 1) * cells]
 
     def edges(it):
         tile_lane = lax.broadcasted_iota(jnp.int32, (cells, 128), 1)
@@ -494,7 +532,7 @@
             end = pltpu.roll(end, planes + z + 1, 1)
             packed = jnp.where(tile_lane == z, begin, packed)
             packed = jnp.where(tile_lane == planes + z, end, packed)
-        turned = dot3((gy_high[...], gy_low[...]), split(packed)).T
+        turned = y_times(*split(packed)).T
         for z in range(planes):
             for side in range(2):
                 total = None
@@ -502,62 +540,77 @@
                     n = side * planes + k
                     term = (KAPPA * z_inv[z, k]) * turned[n : n + 1]
                     total = term if total is None else total + term
-                x_send[it, x_blocks + side : x_blocks + side + 1,
-                       z * cells : (z + 1) * cells] = total
-
-    kept_x = [
-        ends * c + n for c in range(cols) for n in range(ends)
-        if n < x_blocks + 2 or n >= ends - x_blocks
-    ]
+                own_rows[2 * x_blocks + side, z : z + 1, :] = total
+                own_rows[2 * x_blocks + side, planes + z : planes + z + 1, :] = total
+
+    def wide(weights):
+        return jnp.concatenate([weights] * (cells // 128), axis=1)
 
     def x_share(it):
-        own = pl.ds(pl.multiple_of(col * ends, ends), ends)
-        sent = [
-            send(x_send.at[it], x_all.at[it, own, :], x_ssem.at[it, n], x_rsem.at[it, n], col=peer)
+        total = None
+        for n in range(kinds):
+            term = wide(wx_send[n]) * own_rows[n]
+            total = term if total is None else total + term
+        x_send[it] = total
+        x_all[it, col] = total
+        return [
+            send(x_send.at[it], x_all.at[it, col], x_ssem.at[it, n], x_rsem.at[it, n], col=peer)
             for n, peer in enumerate(col_peers)
         ]
-        x_all[it, own, :] = x_send[it]
-        return sent
 
     def y_share(it):
+        sides = []
+        for side in range(2):
+            parts = []
+            for j in range(x_blocks):
+                m = 2 * j + side
+                total = wide(wx_in[m, 0]) * x_all[it, 0]
+                for c in range(1, cols):
+                    total = total + wide(wx_in[m, c]) * x_all[it, c]
+                total = total + pltpu.roll(total, planes, 0)
+                for n in range(kinds):
+                    total = total + wide(wx_own[m, n]) * own_rows[n]
+                parts.append(total)
+            sides.append(jnp.where(upper_wide, parts[0], parts[1]))
         lines = []
-        for z in range(planes):
-            lines.append(weighted(ab_x[...], x_all[it, :, z * cells : (z + 1) * cells], kept_x))
-        for z in range(planes):
-            for top, at in ((0, 0), (1, last)):
-                for j in range(x_blocks):
-                    block = slice(j * cells, (j + 1) * cells)
-                    line = (
-                        mix[z, at : at + 1, block]
-                        + lines[z][2 * j : 2 * j + 1, at : at + 1] * gend[2 * j, :1, :]
-                        + lines[z][2 * j + 1 : 2 * j + 2, at : at + 1] * gend[2 * j + 1, :1, :]
-                    )
-                    y_send[it, 2 * z + top : 2 * z + top + 1, block] = line
-        own = pl.ds(pl.multiple_of(row * 2 * planes, 2 * planes), 2 * planes)
+        for side, at in ((0, 0), (1, last)):
+            line = y_base[side]
+            for n in range(2):
+                scale = jnp.broadcast_to(sides[n][:, at : at + 1], (8, cells))
+                line = line + scale * gend[n, x_blocks]
+            lines.append(line)
+        y_send[it, 0] = lines[1]
+        y_send[it, 1] = lines[0] + wide(wy_turn[...]) * lines[1]
+        y_all[it, row] = lines[1]
         sent = [
-            send(y_send.at[it], y_all.at[it, own, :], y_ssem.at[it, n], y_rsem.at[it, n], row=peer)
+            send(y_send.at[it, lax.div(row + n + 1, rows)], y_all.at[it, row], y_ssem.at[it, n],
+                 y_rsem.at[it, n], row=peer)
             for n, peer in enumerate(row_peers)
         ]
-        y_all[it, own, :] = y_send[it]
-        stacked = jnp.concatenate(
-            lines + [jnp.zeros((128 - 8 * planes, cells), f32)], axis=0
-        ).T
+        stacked = jnp.concatenate(sides + [jnp.zeros((112, cells), f32)], axis=0).T
         for t in range(cells // 8):
             here = slice(t * 8, t * 8 + 8)
             tile = stacked[here]
             for z in range(planes):
                 for j in range(x_blocks):
                     block = slice(j * cells, (j + 1) * cells)
-                    n = 8 * z + 2 * j
+                    n = j * planes + z
                     mix[z, here, block] = (
                         mix[z, here, block]
-                        + tile[:, n : n + 1] * gend[2 * j]
-                        + tile[:, n + 1 : n + 2] * gend[2 * j + 1]
+                        + tile[:, n : n + 1] * gend[0, j]
+                        + tile[:, 8 + n : 9 + n] * gend[1, j]
                     )
         finish(sent)
-        carry = weighted(ab_y[...], y_all[it], range(rows * 2 * planes))
-        for n in range(2 * planes):
-            carry_rows[n] = jnp.broadcast_to(carry[n : n + 1], (8, width))
+        for side in range(2):
+            total = wide(wy_in[side, 0]) * y_all[it, 0]
+            for k in range(1, rows):
+                total = total + wide(wy_in[side, k]) * y_all[it, k]
+            for z in range(planes):
+                for j in range(x_blocks):
+                    n = j * planes + z
+                    carry_rows[2 * z + side, :, j * cells : (j + 1) * cells] = jnp.broadcast_to(
+                        total[n : n + 1], (8, cells)
+                    )
 
     def settle(it, low, high, squares):
         def step(i, acc):
@@ -579,47 +632,53 @@
 
         return lax.fori_loop(low // 8, high // 8, step, squares)
 
+    def stream(it, ready):
+        ready(0)
+        ready(3)
+        shared = share_rows(it)
+        residual(it, 16, cuts[1] - 16)
+        residual(it, cuts[3] + 16, cells - 16)
+        ready(1)
+        residual(it, cuts[1] - 16, cuts[2] - 16)
+        x_product([(16, cuts[2] - 16), (cuts[3] + 16, cells - 16)])
+        ready(2)
+        residual(it, cuts[2] - 16, cuts[3] + 16)
+        finish(shared)
+        mirror(it)
+        residual(it, 0, 16)
+        residual(it, cells - 16, cells)
+        x_product([(0, 16), (cuts[2] - 16, cuts[3] + 16), (cells - 16, cells)])
+        edges(it)
+        y_product()
+
+    def arrived(n):
+        finish(moved_d[n])
+        regroup(cuts[n], cuts[n + 1])
+
+    finish(moved_e)
+    stream(0, arrived)
+    sent = x_share(0)
+    for n in order[2:]:
+        moved_f[n] = move_piece(bound, fz, n, f_ssem, f_rsem)
+    finish(sent)
+    y_share(0)
+
     totals = []
     blank = jnp.zeros((8, width), f32)
-
-    shared = share_rows(0)
-    finish(moved_e)
-    finish(shared)
-    mirror(0)
-    residual(0, 0, cells)
-    products(0)
-    edges(0)
-    sent = x_share(0)
-    for n in range(1, pieces - 1):
-        moved_f[n] = move_bound(n)
+    held = [blank]
+
+    def settled(n):
+        finish(moved_f[n])
+        held.append(settle(0, cuts[n], cuts[n + 1], held.pop()))
+
+    stream(1, settled)
+    sent = x_share(1)
+    totals.append(jnp.sum(held[0]))
     finish(sent)
-    y_share(0)
-
-    squares = blank
-    finish(moved_f[0])
-    squares = settle(0, 0, piece, squares)
-    finish(moved_f[pieces - 1])
-    squares = settle(0, cells - piece, cells, squares)
-    shared = share_rows(1)
-    residual(1, cells - piece + 16, cells - 16)
-    for n in range(1, pieces - 1):
-        finish(moved_f[n])
-        squares = settle(0, n * piece, (n + 1) * piece, squares)
-        low = 16 if n == 1 else n * piece - 16
-        high = (n + 1) * piece - 16
-        residual(1, low, high if n < pieces - 2 else high + 32)
-    totals.append(jnp.sum(squares))
-    finish(shared)
-    mirror(1)
-    residual(1, 0, 16)
-    residual(1, cells - 16, cells)
-    products(1)
-    edges(1)
-    finish(x_share(1))
     y_share(1)
 
     def give_back(n):
-        at = pl.ds(n * piece, piece)
+        at = pl.ds(backs_at[n], backs_at[n + 1] - backs_at[n])
         return [
             send(final.at[peer, at, :], out.at[at, slab(col)], back_ssem.at[n, m],
                  back_rsem.at[n, m], col=peer)
@@ -628,8 +687,8 @@
 
     squares = blank
     backs = []
-    for n in range(pieces):
-        squares = settle(ITERS - 1, n * piece, (n + 1) * piece, squares)
+    for n in range(len(backs_at) - 1):
+        squares = settle(ITERS - 1, backs_at[n], backs_at[n + 1], squares)
         if n < 2:
             backs += give_back(n)
     totals.append(jnp.sum(squares))
@@ -648,12 +707,14 @@
         send(s_col_send, s_col.at[n], sc_ssem.at[n], sc_rsem.at[n], col=peer)
         for n, peer in enumerate(col_peers)
     ]
-    for n in range(2, pieces):
+    for n in range(2, len(backs_at) - 1):
         backs += give_back(n)
     finish(shares)
     for n in range(cols - 1):
         total = total + s_col[n]
-    norms[...] = jnp.sqrt(total / cell_count + EPSILON) / STEP
+    sizes = jnp.sqrt(total / cell_count + EPSILON) / STEP
+    for n in range(ITERS):
+        norms[n] = sizes[n, 0]
     finish(backs)
 
 
@@ -663,9 +724,13 @@
     blocks, _, _ = line_inverses.shape
     width = line_length // cols
     x_blocks = width // cells
-    lines = cols * cells
+    kinds = 2 * x_blocks + 2
     pieces = 4
-    shape = (rows, cols, cells, width, x_blocks, blocks, float(cols * rows * cells * line_length))
+    step = cells // 16
+    cuts = (0, 3 * step, 11 * step, 13 * step, cells)
+    backs_at = tuple(cells * n // pieces for n in range(pieces + 1))
+    cell_count = float(cols * rows * cells * line_length)
+    shape = (rows, cols, cells, width, x_blocks, blocks, cell_count, cuts, backs_at)
     f32 = jnp.float32
     bf16 = jnp.bfloat16
     dma = pltpu.SemaphoreType.DMA
@@ -674,11 +739,11 @@
     damage, norms = pl.pallas_call(
         functools.partial(line_kernel, shape),
         out_shape=(
-            jax.ShapeDtypeStruct((cells, line_length), f32),
-            jax.ShapeDtypeStruct((8, 128), f32),
+            pltpu.VMEM((cells, line_length), f32),
+            jax.ShapeDtypeStruct((ITERS,), f32),
         ),
         in_specs=[smem] + [pl.BlockSpec(memory_space=pl.ANY)] * 5,
-        out_specs=(vmem, vmem),
+        out_specs=(vmem, smem),
         scratch_shapes=[
             pltpu.VMEM((cells, line_length), f32),
             pltpu.VMEM((cells, line_length), jnp.int32),
@@ -692,23 +757,29 @@
             pltpu.VMEM((cols, cells, width), f32),
             pltpu.VMEM((cols, cells, width), bf16),
             pltpu.VMEM((cols, cells, width), bf16),
+            pltpu.VMEM((cols, cells, width), bf16),
+            pltpu.VMEM((cols, cells, width), bf16),
             pltpu.VMEM((cols, cells, width), f32),
             pltpu.VMEM((4, blocks, 8, 128), f32),
             pltpu.VMEM((x_blocks, cells, cells), f32),
             pltpu.VMEM((cells, cells), f32),
             pltpu.VMEM((x_blocks, cells, cells), bf16),
             pltpu.VMEM((x_blocks, cells, cells), bf16),
-            pltpu.VMEM((cells, cells), bf16),
-            pltpu.VMEM((cells, cells), bf16),
+            pltpu.VMEM((2 * cells, cells), bf16),
             pltpu.VMEM((2, cells, 128), f32),
-            pltpu.VMEM((2 * x_blocks, 8, cells), f32),
-            pltpu.VMEM((8, 128), f32),
+            pltpu.VMEM((2, x_blocks + 1, 8, cells), f32),
+            pltpu.VMEM((kinds, 8, 128), f32),
+            pltpu.VMEM((2 * x_blocks, cols, 8, 128), f32),
+            pltpu.VMEM((2 * x_blocks, kinds, 8, 128), f32),
+            pltpu.VMEM((2, rows, 8, 128), f32),
             pltpu.VMEM((8, 128), f32),
             pltpu.VMEM((2 * cols, 8, width), f32),
-            pltpu.VMEM((ITERS, 8, lines), f32),
-            pltpu.VMEM((ITERS, 8 * cols, lines), f32),
-            pltpu.VMEM((ITERS, 2 * cols, width), f32),
-            pltpu.VMEM((ITERS, 2 * cols * rows, width), f32),
+            pltpu.VMEM((kinds, 8, cells), f32),
+            pltpu.VMEM((2, 8, cells), f32),
+            pltpu.VMEM((ITERS, 8, cells), f32),
+            pltpu.VMEM((ITERS, cols, 8, cells), f32),
+            pltpu.VMEM((ITERS, 2, 8, cells), f32),
+            pltpu.VMEM((ITERS, rows, 8, cells), f32),
             pltpu.VMEM((8, 128), f32),
             pltpu.VMEM((rows - 1, 8, 128), f32),
             pltpu.VMEM((8, 128), f32),
@@ -716,8 +787,8 @@
             dma((x_blocks + 9,)),
             dma((cols - 1,)),
             dma((cols - 1,)),
-            dma((cols - 1,)),
-            dma((cols - 1,)),
+            dma((pieces, cols - 1)),
+            dma((pieces, cols - 1)),
             dma((pieces, cols - 1)),
             dma((pieces, cols - 1)),
             dma((pieces, cols - 1)),
@@ -745,7 +816,7 @@
         irreversible[0],
         line_inverses,
     )
-    return damage[None], norms[:ITERS, 0]
+    return damage[None], norms
 
 
 def solution(mesh):
@@ -756,11 +827,10 @@
         whole_blocks = (
             energy.shape[0] == 1
             and energy.shape[1] == block_cells
-            and width % block_cells == 0
-            and 2 * (width // block_cells) + 2 <= 8
-            and block_cells % 128 == 0
+            and width == 2 * block_cells
+            and block_cells % 256 == 0
             and 2 * cols == 8
-            and 8 * max(rows, cols) <= 128
+            and 2 * rows <= 128
             and min(rows, cols) > 2
         )
         chosen = local if whole_blocks else local_turned

time: 126 us -> 116 us (0.921)
  Pallas kernels: 121 us -> 114 us
  local copies, waits for them, and re-layouts: 4.45 us -> 1.84 us
    pallas_call x1, Pallas kernels: 121 us -> 114 us  [local(): pl.pallas_call(functools.partial(line_kernel, shape), out_shape=(pltpu.VM...]
    slice x1 -> x0, local copies, waits for them, and re-layouts: 1.31 us -> none  [local(): return (damage[None], norms[:ITERS, 0])]
    unnamed x1 -> x4, local copies, waits for them, and re-layouts: 3.13 us -> 1.84 us
where the time goes in v2:
time: 116 us
  Pallas kernels  114 us (98%)
  local copies, waits for them, and re-layouts  1.84 us (2%)
    pallas_call x1, Pallas kernels, local(): pl.pallas_call(functools.partial(line_kernel, shape), out_shape=(pltpu.VM...  114 us

profile of v2, /device:TPU:0, one launch (start us, length us, event | category | flops | bytes accessed | tf_op | source)
XLA Modules:
  0.0 116.3 jit_solution(1643805332873499440)
XLA Ops:
  0.6 113.8 %line_iterations.1 = (f32[256,2048]{1,0:T(8,128)S(1)}, f32[2]{0:T(128)}) custom-call(f32[4,4]{1,0:T(4,128)} %z_inv.1, f32[256,2048]{1,0:T(8,128)} %bitcast.6, f32[256,2048]{1,0:T(8,128)} %bitcast.7, s32[256,2048]{1,0:T(8,128)} %bitcast.8, s32[256,2048]{1,0:T(8,128)} %bitcast.9, f32[8,256,256]{2,1,0:T(8,128)} %inverses.1), custom_call_target="tpu_custom_call" | custom-call | tf_op jit(solution)/shard_map/line_iterations/pallas_call | solution.py:739
  114.4 0.0 copy-start
  114.4 1.3 %copy.10 = f32[1,256,2048]{2,1,0:T(8,128)} copy(f32[1,256,2048]{2,1,0:T(8,128)S(1)} %bitcast.5) | data formatting | bytes 4194304
  115.7 0.0 copy-done
  115.7 0.5 copy.11
Async XLA Ops:
  114.4 1.3 %copy-start = (f32[2]{0:T(128)S(1)}, f32[2]{0:T(128)}, u32[]{:S(2)}) copy-start(f32[2]{0:T(128)} %get-tuple-element.11) | copy-start | bytes 28

commit v3 on v2

--- a/solution.py
+++ b/solution.py
@@ -127,7 +127,7 @@
 
 def line_kernel(
     shape,
-    z_inv,
+    z_hbm,
     energy,
     damage_hbm,
     seeds_hbm,
@@ -141,6 +141,7 @@
     start,
     bound,
     ez,
+    ec,
     fz,
     landing,
     dz,
@@ -165,6 +166,8 @@
     wy_turn,
     carry_rows,
     own_rows,
+    packed,
+    w_mix,
     y_base,
     x_send,
     x_all,
@@ -174,6 +177,7 @@
     s_row,
     s_col_send,
     s_col,
+    z_inv,
     local_sems,
     e_ssem,
     e_rsem,
@@ -229,19 +233,6 @@
     def dot(a, b):
         return jnp.dot(a, b, preferred_element_type=f32)
 
-    def line_ends(field):
-        tile_lane = lax.broadcasted_iota(jnp.int32, (cells, 128), 1)
-        packed = field[:, :128]
-        for j in range(x_blocks):
-            begin = field[:, j * cells : j * cells + 128]
-            end = field[:, (j + 1) * cells - 128 : (j + 1) * cells]
-            if j > 0:
-                begin = pltpu.roll(begin, j, 1)
-                packed = jnp.where(tile_lane == j, begin, packed)
-            end = pltpu.roll(end, x_blocks + j + 1, 1)
-            packed = jnp.where(tile_lane == x_blocks + j, end, packed)
-        return packed.T[:8]
-
     barrier = pltpu.get_barrier_semaphore()
     for peer in col_peers:
         pl.semaphore_signal(
@@ -260,6 +251,7 @@
     fetch = [
         pltpu.make_async_copy(energy.at[:, slab(col)], ez.at[col], local_sems.at[3]),
         pltpu.make_async_copy(inverses.at[row], gy, local_sems.at[4]),
+        pltpu.make_async_copy(z_hbm, z_inv, local_sems.at[9 + x_blocks]),
     ]
     for n in range(4):
         down, over = (cells - 8) * (n // 2), (cells - 128) * (n % 2)
@@ -298,7 +290,7 @@
         start[at, :] = jnp.where(seeded, 1.0, old)
         bound[at, :] = jnp.where(seeded, 1.0, jnp.where(irreversible[at, :] == 1, old, 0.0))
 
-    order = (0, 3, 1, 2)
+    order = (0, 4, 1, 2, 3)
     moved_d = {n: move_piece(start, landing, n, d_ssem, d_rsem) for n in order}
     moved_f = {n: move_piece(bound, fz, n, f_ssem, f_rsem) for n in order[:2]}
     landing[col] = start[:, slab(col)]
@@ -426,6 +418,22 @@
     lane16 = lax.broadcasted_iota(jnp.int32, (16, 128), 1)
     at_first, at_last = lane16 == 0, lane16 == 127
 
+    mixing = [[KAPPA * z_inv[z, k] for k in range(planes)] for z in range(planes)]
+    for k in range(planes):
+        weights = zero
+        for z in range(planes):
+            weights = jnp.where(lax.rem(sub, planes) == z, mixing[z][k], weights)
+        w_mix[k] = weights
+
+    def scale_energy():
+        @pl.loop(0, cells // 8)
+        def _(i):
+            for z in range(planes):
+                sides = 4 + (z > 0) + (z < planes - 1)
+                scaled = ez[z, eight(i * 8), :] * (1.0 / KAPPA)
+                ez[z, eight(i * 8), :] = scaled
+                ec[z, eight(i * 8), :] = scaled + (1.0 / KAPPA + sides)
+
     def regroup(low, high):
         @pl.loop(low // 8, high // 8)
         def _(i):
@@ -475,34 +483,52 @@
                         after = pltpu.roll(dz[it, z, g + 1, padded, :], 127, 1)
                     near = near + jnp.where(at_first, before, pltpu.roll(d, 1, 1))
                     near = near + jnp.where(at_last, after, pltpu.roll(d, 127, 1))
-                    sides = 4
                     if z > 0:
                         near = near + mids[z - 1]
-                        sides += 1
                     if z < planes - 1:
                         near = near + mids[z + 1]
-                        sides += 1
-                    e = ez[z, here, lanes]
-                    value.append((e - (e + (1.0 + KAPPA * sides)) * d) + KAPPA * near)
+                    value.append(near + (ez[z, here, lanes] - ec[z, here, lanes] * d))
                 for z in range(planes):
-                    total = z_inv[z, 0] * value[0]
+                    total = mixing[z][0] * value[0]
                     for k in range(1, planes):
-                        total = total + z_inv[z, k] * value[k]
+                        total = total + mixing[z][k] * value[k]
                     w_high[z, here, lanes], w_low[z, here, lanes] = split(total)
 
-    def x_product(ranges):
+    def x_product(it, ranges):
+        packs = [jnp.zeros((b - a, 128), f32) for a, b in ranges]
+        spots = [lax.broadcasted_iota(jnp.int32, (b - a, 128), 1) for a, b in ranges]
+
+        def place(n, tile, lane_from, lane_to):
+            if lane_from != lane_to:
+                tile = pltpu.roll(tile, (lane_to - lane_from) % 128, 1)
+            packs[n] = jnp.where(spots[n] == lane_to, tile, packs[n])
+
         for j in range(x_blocks):
             block = slice(j * cells, (j + 1) * cells)
-            parts = [(z, low, high) for z in range(planes) for low, high in ranges]
-            high_rows = jnp.concatenate([w_high[z, a:b, block] for z, a, b in parts], axis=0)
-            low_rows = jnp.concatenate([w_low[z, a:b, block] for z, a, b in parts], axis=0)
+            parts = [(z, n) for z in range(planes) for n in range(len(ranges))]
+            cut = [slice(*ranges[n]) for _, n in parts]
+            high_rows = jnp.concatenate(
+                [w_high[z, c, block] for (z, _), c in zip(parts, cut)], axis=0
+            )
+            low_rows = jnp.concatenate(
+                [w_low[z, c, block] for (z, _), c in zip(parts, cut)], axis=0
+            )
             count = high_rows.shape[0]
             twice = dot(jnp.concatenate([high_rows, low_rows], axis=0), gx_high[j])
             along = twice[:count] + (twice[count:] + dot(high_rows, gx_low[j]))
             at = 0
-            for z, a, b in parts:
-                a_high[z, a:b, block], a_low[z, a:b, block] = split(along[at : at + b - a])
-                at += b - a
+            for (z, n), c in zip(parts, cut):
+                part = along[at : at + c.stop - c.start]
+                at += c.stop - c.start
+                a_high[z, c, block], a_low[z, c, block] = split(part)
+                place(n, part[:, :128], 0, j * planes + z)
+                place(n, part[:, cells - 128 :], 127, (x_blocks + j) * planes + z)
+        for n, (a, b) in enumerate(ranges):
+            for z in range(planes):
+                near = pl.ds(8 + a, b - a)
+                place(n, dz[it, z, 0, near, :], 0, 2 * x_blocks * planes + z)
+                place(n, dz[it, z, groups - 1, near, :], 127, (2 * x_blocks + 1) * planes + z)
+            packed[a:b, :] = packs[n]
 
     def y_times(high, low):
         twice = dot(gy_both[...], high)
@@ -512,36 +538,33 @@
         for z in range(planes):
             both = y_times(a_high[z], a_low[z])
             mix[z] = both
-            turned = line_ends(both)
-            for n in range(2 * x_blocks):
-                own_rows[n, z : z + 1, :] = turned[n : n + 1]
-                own_rows[n, planes + z : planes + z + 1, :] = turned[n : n + 1]
             for side, at in ((0, 0), (1, last)):
                 for j in range(x_blocks):
                     n = j * planes + z
                     y_base[side, n : n + 1, :] = both[at : at + 1, j * cells : (j + 1) * cells]
 
-    def edges(it):
-        tile_lane = lax.broadcasted_iota(jnp.int32, (cells, 128), 1)
-        packed = jnp.zeros((cells, 128), f32)
-        for z in range(planes):
-            begin = dz[it, z, 0, pl.ds(8, cells), :]
-            end = dz[it, z, groups - 1, pl.ds(8, cells), :]
-            if z > 0:
-                begin = pltpu.roll(begin, z, 1)
-            end = pltpu.roll(end, planes + z + 1, 1)
-            packed = jnp.where(tile_lane == z, begin, packed)
-            packed = jnp.where(tile_lane == planes + z, end, packed)
-        turned = y_times(*split(packed)).T
-        for z in range(planes):
-            for side in range(2):
-                total = None
-                for k in range(planes):
-                    n = side * planes + k
-                    term = (KAPPA * z_inv[z, k]) * turned[n : n + 1]
-                    total = term if total is None else total + term
-                own_rows[2 * x_blocks + side, z : z + 1, :] = total
-                own_rows[2 * x_blocks + side, planes + z : planes + z + 1, :] = total
+    def x_ends():
+        turned = y_times(*split(packed[...])).T
+
+        def keep(n, tile):
+            other = pltpu.roll(tile, planes, 0)
+            pair = (tile, other) if n % 2 == 0 else (other, tile)
+            own_rows[n] = jnp.where(upper_wide, pair[0], pair[1])
+
+        for n in range(2 * x_blocks):
+            keep(n, turned[8 * (n // 2) : 8 * (n // 2) + 8])
+        tile = turned[8 * x_blocks : 8 * x_blocks + 8]
+        total = None
+        for k in range(planes):
+            line = jnp.where(
+                upper_wide,
+                jnp.broadcast_to(tile[k : k + 1], (8, cells)),
+                jnp.broadcast_to(tile[planes + k : planes + k + 1], (8, cells)),
+            )
+            term = wide(w_mix[k]) * line
+            total = term if total is None else total + term
+        for n in range(2):
+            keep(2 * x_blocks + n, total)
 
     def wide(weights):
         return jnp.concatenate([weights] * (cells // 128), axis=1)
@@ -633,33 +656,35 @@
         return lax.fori_loop(low // 8, high // 8, step, squares)
 
     def stream(it, ready):
-        ready(0)
-        ready(3)
+        ready(order[0])
+        ready(order[1])
         shared = share_rows(it)
-        residual(it, 16, cuts[1] - 16)
-        residual(it, cuts[3] + 16, cells - 16)
-        ready(1)
-        residual(it, cuts[1] - 16, cuts[2] - 16)
-        x_product([(16, cuts[2] - 16), (cuts[3] + 16, cells - 16)])
-        ready(2)
-        residual(it, cuts[2] - 16, cuts[3] + 16)
         finish(shared)
         mirror(it)
-        residual(it, 0, 16)
-        residual(it, cells - 16, cells)
-        x_product([(0, 16), (cuts[2] - 16, cuts[3] + 16), (cells - 16, cells)])
-        edges(it)
-        y_product()
+        ranges = [(0, cuts[1] - 16), (cuts[4] + 16, cells)]
+        for a, b in ranges:
+            residual(it, a, b)
+        x_product(it, ranges)
+        for n in order[2:]:
+            ready(n)
+            a, b = cuts[n] - 16, cuts[n + 1] - 16
+            if n == order[-1]:
+                b += 32
+            residual(it, a, b)
+            x_product(it, [(a, b)])
+        x_ends()
 
     def arrived(n):
         finish(moved_d[n])
         regroup(cuts[n], cuts[n + 1])
 
     finish(moved_e)
+    scale_energy()
     stream(0, arrived)
     sent = x_share(0)
     for n in order[2:]:
         moved_f[n] = move_piece(bound, fz, n, f_ssem, f_rsem)
+    y_product()
     finish(sent)
     y_share(0)
 
@@ -673,6 +698,7 @@
 
     stream(1, settled)
     sent = x_share(1)
+    y_product()
     totals.append(jnp.sum(held[0]))
     finish(sent)
     y_share(1)
@@ -713,8 +739,7 @@
     for n in range(cols - 1):
         total = total + s_col[n]
     sizes = jnp.sqrt(total / cell_count + EPSILON) / STEP
-    for n in range(ITERS):
-        norms[n] = sizes[n, 0]
+    norms[...] = jnp.where(lane == 0, sizes[:1, :], sizes[1:2, :])[0, :ITERS]
     finish(backs)
 
 
@@ -727,7 +752,7 @@
     kinds = 2 * x_blocks + 2
     pieces = 4
     step = cells // 16
-    cuts = (0, 3 * step, 11 * step, 13 * step, cells)
+    cuts = (0, 3 * step, 8 * step, 12 * step, 13 * step, cells)
     backs_at = tuple(cells * n // pieces for n in range(pieces + 1))
     cell_count = float(cols * rows * cells * line_length)
     shape = (rows, cols, cells, width, x_blocks, blocks, cell_count, cuts, backs_at)
@@ -735,21 +760,21 @@
     bf16 = jnp.bfloat16
     dma = pltpu.SemaphoreType.DMA
     vmem = pl.BlockSpec(memory_space=pltpu.VMEM)
-    smem = pl.BlockSpec(memory_space=pltpu.SMEM)
     damage, norms = pl.pallas_call(
         functools.partial(line_kernel, shape),
         out_shape=(
             pltpu.VMEM((cells, line_length), f32),
-            jax.ShapeDtypeStruct((ITERS,), f32),
+            pltpu.VMEM((ITERS,), f32),
         ),
-        in_specs=[smem] + [pl.BlockSpec(memory_space=pl.ANY)] * 5,
-        out_specs=(vmem, smem),
+        in_specs=[pl.BlockSpec(memory_space=pl.ANY)] * 6,
+        out_specs=(vmem, vmem),
         scratch_shapes=[
             pltpu.VMEM((cells, line_length), f32),
             pltpu.VMEM((cells, line_length), jnp.int32),
             pltpu.VMEM((cells, line_length), jnp.int32),
             pltpu.VMEM((cells, line_length), f32),
             pltpu.VMEM((cells, line_length), f32),
+            pltpu.VMEM((cols, cells, width), f32),
             pltpu.VMEM((cols, cells, width), f32),
             pltpu.VMEM((cols, cells, width), f32),
             pltpu.VMEM((cols, cells, width), f32),
@@ -775,6 +800,8 @@
             pltpu.VMEM((8, 128), f32),
             pltpu.VMEM((2 * cols, 8, width), f32),
             pltpu.VMEM((kinds, 8, cells), f32),
+            pltpu.VMEM((cells, 128), f32),
+            pltpu.VMEM((cols, 8, 128), f32),
             pltpu.VMEM((2, 8, cells), f32),
             pltpu.VMEM((ITERS, 8, cells), f32),
             pltpu.VMEM((ITERS, cols, 8, cells), f32),
@@ -784,13 +811,14 @@
             pltpu.VMEM((rows - 1, 8, 128), f32),
             pltpu.VMEM((8, 128), f32),
             pltpu.VMEM((cols - 1, 8, 128), f32),
-            dma((x_blocks + 9,)),
+            pltpu.SMEM((cols, cols), f32),
+            dma((x_blocks + 10,)),
             dma((cols - 1,)),
             dma((cols - 1,)),
-            dma((pieces, cols - 1)),
-            dma((pieces, cols - 1)),
-            dma((pieces, cols - 1)),
-            dma((pieces, cols - 1)),
+            dma((5, cols - 1)),
+            dma((5, cols - 1)),
+            dma((5, cols - 1)),
+            dma((5, cols - 1)),
             dma((pieces, cols - 1)),
             dma((pieces, cols - 1)),
             dma((ITERS, cols - 1)),

time: 116 us -> 114 us (0.983)
  Pallas kernels: 114 us -> 111 us
    pallas_call x1, Pallas kernels: 114 us -> 111 us  [local(): pl.pallas_call(functools.partial(line_kernel, shape), out_shape=(pltpu.VM...]
where the time goes in v3:
time: 114 us; the launch traced here: 113 us
  Pallas kernels  111 us (97%)
  local copies, waits for them, and re-layouts  1.83 us (2%)
    pallas_call x1, Pallas kernels, local(): pl.pallas_call(functools.partial(line_kernel, shape), out_shape=(pltpu.VM...  111 us

profile of v3, /device:TPU:0, one launch (start us, length us, event | category | flops | bytes accessed | tf_op | source)
XLA Modules:
  0.0 113.5 jit_solution(16580912987525888058)
XLA Ops:
  0.6 111.0 %line_iterations.1 = (f32[256,2048]{1,0:T(8,128)S(1)}, f32[2]{0:T(128)S(1)}) custom-call(f32[4,4]{1,0:T(4,128)} %z_hbm.1, f32[256,2048]{1,0:T(8,128)} %bitcast.6, f32[256,2048]{1,0:T(8,128)} %bitcast.7, s32[256,2048]{1,0:T(8,128)} %bitcast.8, s32[256,2048]{1,0:T(8,128)} %bitcast.9, f32[8,256,256]{2,1,0:T(8,128)} %inverses.1), custom_call_target="tpu_custom_call" | custom-call | tf_op jit(solution)/shard_map/line_iterations/pallas_call | solution.py:763
  111.6 1.3 %copy.10 = f32[1,256,2048]{2,1,0:T(8,128)} copy(f32[1,256,2048]{2,1,0:T(8,128)S(1)} %bitcast.5) | data formatting | bytes 4194304
  113.0 0.5 copy.11

commit v4 on v3

--- a/solution.py
+++ b/solution.py
@@ -169,6 +169,12 @@
     packed,
     w_mix,
     y_base,
+    strips,
+    g_all,
+    word_send,
+    word_all,
+    x_cols,
+    y_lines,
     x_send,
     x_all,
     y_send,
@@ -187,6 +193,8 @@
     f_rsem,
     back_ssem,
     back_rsem,
+    w_ssem,
+    w_rsem,
     x_ssem,
     x_rsem,
     v_ssem,
@@ -263,6 +271,12 @@
     for j in range(x_blocks):
         fetch.append(
             pltpu.make_async_copy(inverses.at[col * x_blocks + j], gx.at[j], local_sems.at[9 + j])
+        )
+    for side, at in ((0, 0), (1, cells - 128)):
+        fetch.append(
+            pltpu.make_async_copy(
+                inverses.at[:, :, pl.ds(at, 128)], strips.at[side], local_sems.at[10 + x_blocks + side]
+            )
         )
     for copy in pulls + fetch:
         copy.start()
@@ -412,6 +426,11 @@
     gy_both[:cells], gy_both[cells:] = split(gy[...])
     gy_ends[0] = jnp.broadcast_to(gy[:, :1], (cells, 128))
     gy_ends[1] = jnp.broadcast_to(gy[:, last:], (cells, 128))
+
+    for k in range(blocks):
+        for side, at in ((0, 0), (1, 127)):
+            line = strips[side, k].T[at : at + 1]
+            g_all[side, k] = jnp.broadcast_to(line, (8, cells))
 
     first_col = jnp.where(col == 0, 1.0, 0.0)
     last_col = jnp.where(col == cols - 1, 1.0, 0.0)
@@ -534,14 +553,15 @@
         twice = dot(gy_both[...], high)
         return twice[:cells] + (twice[cells:] + dot(gy_both[:cells], low))
 
-    def y_product():
-        for z in range(planes):
-            both = y_times(a_high[z], a_low[z])
-            mix[z] = both
-            for side, at in ((0, 0), (1, last)):
-                for j in range(x_blocks):
-                    n = j * planes + z
-                    y_base[side, n : n + 1, :] = both[at : at + 1, j * cells : (j + 1) * cells]
+    def y_product(it, z):
+        both = y_times(a_high[z], a_low[z])
+        mix[z] = both
+        for side, at in ((0, 0), (1, last)):
+            for j in range(x_blocks):
+                y_base[side, z, j : j + 1, :] = both[at : at + 1, j * cells : (j + 1) * cells]
+        if it + 1 == ITERS:
+            d = jnp.concatenate([dz[it, z, g, pl.ds(8, cells), :] for g in range(groups)], axis=1)
+            final[z] = d + STEP * both
 
     def x_ends():
         turned = y_times(*split(packed[...])).T
@@ -597,7 +617,10 @@
             sides.append(jnp.where(upper_wide, parts[0], parts[1]))
         lines = []
         for side, at in ((0, 0), (1, last)):
-            line = y_base[side]
+            line = jnp.concatenate(
+                [y_base[side, z, j : j + 1, :] for j in range(x_blocks) for z in range(planes)],
+                axis=0,
+            )
             for n in range(2):
                 scale = jnp.broadcast_to(sides[n][:, at : at + 1], (8, cells))
                 line = line + scale * gend[n, x_blocks]
@@ -624,6 +647,7 @@
                         + tile[:, 8 + n : 9 + n] * gend[1, j]
                     )
         finish(sent)
+        carried = []
         for side in range(2):
             total = wide(wy_in[side, 0]) * y_all[it, 0]
             for k in range(1, rows):
@@ -634,6 +658,8 @@
                     carry_rows[2 * z + side, :, j * cells : (j + 1) * cells] = jnp.broadcast_to(
                         total[n : n + 1], (8, cells)
                     )
+            carried.append(total)
+        return sides, carried
 
     def settle(it, low, high, squares):
         def step(i, acc):
@@ -647,8 +673,6 @@
                 if it + 1 < ITERS:
                     for g in range(groups):
                         dz[it + 1, z, g, padded, :] = renewed[:, g * 128 : (g + 1) * 128]
-                else:
-                    final[z, here, :] = renewed
                 change = renewed - d
                 acc = acc + change * change
             return acc
@@ -684,7 +708,8 @@
     sent = x_share(0)
     for n in order[2:]:
         moved_f[n] = move_piece(bound, fz, n, f_ssem, f_rsem)
-    y_product()
+    for z in range(planes):
+        y_product(0, z)
     finish(sent)
     y_share(0)
 
@@ -697,33 +722,66 @@
         held.append(settle(0, cuts[n], cuts[n + 1], held.pop()))
 
     stream(1, settled)
+    def give_back(n, m):
+        at = pl.ds(backs_at[n], backs_at[n + 1] - backs_at[n])
+        return send(final.at[col_peers[m], at, :], out.at[at, slab(col)], back_ssem.at[n, m],
+                    back_rsem.at[n, m], col=col_peers[m])
+
+    backs = [[] for _ in backs_at[1:]]
+
+    def give_all(n):
+        for m in range(cols - 1):
+            backs[n].append(give_back(n, m))
+
+    def complete(low, high):
+        @pl.loop(low // 8, high // 8)
+        def _(i):
+            here = eight(i * 8)
+            tile = x_cols[here, :]
+            ends_of = [
+                jnp.concatenate([gy_ends[n, here, :]] * (cells // 128), axis=1) for n in range(2)
+            ]
+            for k in range(blocks):
+                block = slice(k * cells, (k + 1) * cells)
+                n = 8 * (k // x_blocks) + 2 * (k % x_blocks)
+                value = (
+                    out[here, block]
+                    + tile[:, n : n + 1] * g_all[0, k]
+                    + tile[:, n + 1 : n + 2] * g_all[1, k]
+                    + (ends_of[0] * y_lines[0, k] + ends_of[1] * y_lines[1, k])
+                )
+                out[here, block] = jnp.minimum(jnp.maximum(value, bound[here, block]), 1.0)
+
     sent = x_share(1)
-    y_product()
+    for m in range(cols - 1):
+        y_product(1, col_peers[m])
+        for n in range(2):
+            backs[n].append(give_back(n, m))
+    y_product(1, col)
+    out[:, slab(col)] = final[col]
+    finish(sent)
+    sides, carried = y_share(1)
+    for z in range(planes):
+        for j in range(x_blocks):
+            n = j * planes + z
+            for side in range(2):
+                at = 2 * j + side
+                word_send[z, at : at + 1, :] = STEP * sides[side][n : n + 1]
+                at += 2 * x_blocks
+                word_send[z, at : at + 1, :] = STEP * carried[side][n : n + 1]
+    words = [
+        send(word_send.at[peer], word_all.at[col], w_ssem.at[n], w_rsem.at[n], col=peer)
+        for n, peer in enumerate(col_peers)
+    ]
+    give_all(2)
+    word_all[col] = word_send[col]
     totals.append(jnp.sum(held[0]))
-    finish(sent)
-    y_share(1)
-
-    def give_back(n):
-        at = pl.ds(backs_at[n], backs_at[n + 1] - backs_at[n])
-        return [
-            send(final.at[peer, at, :], out.at[at, slab(col)], back_ssem.at[n, m],
-                 back_rsem.at[n, m], col=peer)
-            for m, peer in enumerate(col_peers)
-        ]
-
-    squares = blank
-    backs = []
-    for n in range(len(backs_at) - 1):
-        squares = settle(ITERS - 1, backs_at[n], backs_at[n + 1], squares)
-        if n < 2:
-            backs += give_back(n)
-    totals.append(jnp.sum(squares))
+    totals.append(jnp.sum(settle(ITERS - 1, 0, cells, blank)))
     s_send[...] = jnp.where(sub == 0, totals[0], jnp.where(sub == 1, totals[1], 0.0))
     shares = [
         send(s_send, s_row.at[n], sr_ssem.at[n], sr_rsem.at[n], row=peer)
         for n, peer in enumerate(row_peers)
     ]
-    out[:, slab(col)] = final[col]
     finish(shares)
     total = s_send[...]
     for n in range(rows - 1):
@@ -733,14 +791,28 @@
         send(s_col_send, s_col.at[n], sc_ssem.at[n], sc_rsem.at[n], col=peer)
         for n, peer in enumerate(col_peers)
     ]
-    for n in range(2, len(backs_at) - 1):
-        backs += give_back(n)
+    for n in range(3, len(backs_at) - 1):
+        give_all(n)
+    finish(words)
+    x_cols[...] = jnp.concatenate(
+        [word_all[c] for c in range(cols)] + [jnp.zeros((128 - 8 * cols, cells), f32)], axis=0
+    ).T
+    for k in range(blocks):
+        for side in range(2):
+            at = 2 * x_blocks + 2 * (k % x_blocks) + side
+            y_lines[side, k] = jnp.broadcast_to(
+                word_all[k // x_blocks, at : at + 1, :], (8, cells)
+            )
+    for n in range(len(backs_at) - 2):
+        finish(backs[n])
+        complete(backs_at[n], backs_at[n + 1])
     finish(shares)
     for n in range(cols - 1):
         total = total + s_col[n]
     sizes = jnp.sqrt(total / cell_count + EPSILON) / STEP
     norms[...] = jnp.where(lane == 0, sizes[:1, :], sizes[1:2, :])[0, :ITERS]
-    finish(backs)
+    finish(backs[-1])
+    complete(backs_at[-2], backs_at[-1])
 
 
 def local(energy, damage_old, crack_seeds, irreversible, line_inverses, z_inverse):
@@ -750,10 +822,9 @@
     width = line_length // cols
     x_blocks = width // cells
     kinds = 2 * x_blocks + 2
-    pieces = 4
     step = cells // 16
     cuts = (0, 3 * step, 8 * step, 12 * step, 13 * step, cells)
-    backs_at = tuple(cells * n // pieces for n in range(pieces + 1))
+    backs_at = (0, 4 * step, 8 * step, 11 * step, 14 * step, cells)
     cell_count = float(cols * rows * cells * line_length)
     shape = (rows, cols, cells, width, x_blocks, blocks, cell_count, cuts, backs_at)
     f32 = jnp.float32
@@ -802,7 +873,13 @@
             pltpu.VMEM((kinds, 8, cells), f32),
             pltpu.VMEM((cells, 128), f32),
             pltpu.VMEM((cols, 8, 128), f32),
-            pltpu.VMEM((2, 8, cells), f32),
+            pltpu.VMEM((2, cols, 8, cells), f32),
+            pltpu.VMEM((2, blocks, cells, 128), f32),
+            pltpu.VMEM((2, blocks, 8, cells), f32),
+            pltpu.VMEM((cols, 8, cells), f32),
+            pltpu.VMEM((cols, 8, cells), f32),
+            pltpu.VMEM((cells, 128), f32),
+            pltpu.VMEM((2, blocks, 8, cells), f32),
             pltpu.VMEM((ITERS, 8, cells), f32),
             pltpu.VMEM((ITERS, cols, 8, cells), f32),
             pltpu.VMEM((ITERS, 2, 8, cells), f32),
@@ -812,15 +889,17 @@
             pltpu.VMEM((8, 128), f32),
             pltpu.VMEM((cols - 1, 8, 128), f32),
             pltpu.SMEM((cols, cols), f32),
-            dma((x_blocks + 10,)),
+            dma((x_blocks + 12,)),
             dma((cols - 1,)),
             dma((cols - 1,)),
             dma((5, cols - 1)),
             dma((5, cols - 1)),
             dma((5, cols - 1)),
             dma((5, cols - 1)),
-            dma((pieces, cols - 1)),
-            dma((pieces, cols - 1)),
+            dma((5, cols - 1)),
+            dma((5, cols - 1)),
+            dma((cols - 1,)),
+            dma((cols - 1,)),
             dma((ITERS, cols - 1)),
             dma((ITERS, cols - 1)),
             dma((ITERS, 2)),

time: 114 us -> 108 us (0.947)
  Pallas kernels: 111 us -> 105 us
    pallas_call x1, Pallas kernels: 111 us -> 105 us  [local(): pl.pallas_call(functools.partial(line_kernel, shape), out_shape=(pltpu.VM...]
where the time goes in v4:
time: 108 us
  Pallas kernels  105 us (97%)
  local copies, waits for them, and re-layouts  1.83 us (2%)
    pallas_call x1, Pallas kernels, local(): pl.pallas_call(functools.partial(line_kernel, shape), out_shape=(pltpu.VM...  105 us

profile of v4, /device:TPU:0, one launch (start us, length us, event | category | flops | bytes accessed | tf_op | source)
XLA Modules:
  0.0 107.6 jit_solution(13338536590743920610)
XLA Ops:
  0.6 105.2 %line_iterations.1 = (f32[256,2048]{1,0:T(8,128)S(1)}, f32[2]{0:T(128)S(1)}) custom-call(f32[4,4]{1,0:T(4,128)} %z_hbm.1, f32[256,2048]{1,0:T(8,128)} %bitcast.6, f32[256,2048]{1,0:T(8,128)} %bitcast.7, s32[256,2048]{1,0:T(8,128)} %bitcast.8, s32[256,2048]{1,0:T(8,128)} %bitcast.9, f32[8,256,256]{2,1,0:T(8,128)} %inverses.1), custom_call_target="tpu_custom_call" | custom-call | tf_op jit(solution)/shard_map/line_iterations/pallas_call | solution.py:834
  105.8 1.3 %copy.10 = f32[1,256,2048]{2,1,0:T(8,128)} copy(f32[1,256,2048]{2,1,0:T(8,128)S(1)} %bitcast.5) | data formatting | bytes 4194304
  107.1 0.5 copy.11

commit v5 on v4

--- a/solution.py
+++ b/solution.py
@@ -151,9 +151,7 @@
     a_high,
     a_low,
     mix,
-    corner,
-    gx,
-    gy,
+    inverse,
     gx_high,
     gx_low,
     gy_both,
@@ -169,7 +167,6 @@
     packed,
     w_mix,
     y_base,
-    strips,
     g_all,
     word_send,
     word_all,
@@ -185,26 +182,19 @@
     s_col,
     z_inv,
     local_sems,
-    e_ssem,
-    e_rsem,
+    greet,
+    e_sems,
     d_ssem,
     d_rsem,
     f_ssem,
     f_rsem,
     back_ssem,
     back_rsem,
-    w_ssem,
-    w_rsem,
-    x_ssem,
-    x_rsem,
-    v_ssem,
-    v_rsem,
-    y_ssem,
-    y_rsem,
-    sc_ssem,
-    sc_rsem,
-    sr_ssem,
-    sr_rsem,
+    w_sems,
+    x_sems,
+    v_sems,
+    y_sems,
+    s_sems,
 ):
     rows, cols, cells, width, x_blocks, blocks, cell_count, cuts, backs_at = shape
     planes = cols
@@ -230,9 +220,8 @@
         copy.start()
         return copy
 
-    def finish(sent):
-        for copy in sent:
-            copy.wait()
+    def finish(sem, sized):
+        pltpu.make_async_copy(sized, sized, sem).wait()
 
     def split(a):
         high = a.astype(jnp.bfloat16)
@@ -246,10 +235,20 @@
         pl.semaphore_signal(
             barrier, inc=1, device_id={"col": peer}, device_id_type=pl.DeviceIdType.MESH
         )
-    for peer in row_peers:
+    above, below = row > 0, row < rows - 1
+
+    def signal_row(sem, who):
         pl.semaphore_signal(
-            barrier, inc=1, device_id={"row": peer}, device_id_type=pl.DeviceIdType.MESH
+            sem, inc=1, device_id={"row": who}, device_id_type=pl.DeviceIdType.MESH
         )
+
+    @pl.when(above)
+    def _():
+        signal_row(barrier, row - 1)
+
+    @pl.when(below)
+    def _():
+        signal_row(barrier, row + 1)
 
     pulls = [
         pltpu.make_async_copy(damage_hbm, damage_old, local_sems.at[0]),
@@ -258,43 +257,28 @@
     ]
     fetch = [
         pltpu.make_async_copy(energy.at[:, slab(col)], ez.at[col], local_sems.at[3]),
-        pltpu.make_async_copy(inverses.at[row], gy, local_sems.at[4]),
-        pltpu.make_async_copy(z_hbm, z_inv, local_sems.at[9 + x_blocks]),
+        pltpu.make_async_copy(inverses, inverse, local_sems.at[4]),
+        pltpu.make_async_copy(z_hbm, z_inv, local_sems.at[5]),
     ]
-    for n in range(4):
-        down, over = (cells - 8) * (n // 2), (cells - 128) * (n % 2)
-        fetch.append(
-            pltpu.make_async_copy(
-                inverses.at[:, pl.ds(down, 8), pl.ds(over, 128)], corner.at[n], local_sems.at[5 + n]
-            )
-        )
-    for j in range(x_blocks):
-        fetch.append(
-            pltpu.make_async_copy(inverses.at[col * x_blocks + j], gx.at[j], local_sems.at[9 + j])
-        )
-    for side, at in ((0, 0), (1, cells - 128)):
-        fetch.append(
-            pltpu.make_async_copy(
-                inverses.at[:, :, pl.ds(at, 128)], strips.at[side], local_sems.at[10 + x_blocks + side]
-            )
-        )
     for copy in pulls + fetch:
         copy.start()
-    pl.semaphore_wait(barrier, rows + cols - 2)
+    neighbours = jnp.where(above, 1, 0) + jnp.where(below, 1, 0)
+    pl.semaphore_wait(barrier, cols - 1 + neighbours)
 
     def move_piece(src, target, index, ssem, rsem):
         at = pl.ds(cuts[index], cuts[index + 1] - cuts[index])
-        return [
-            send(src.at[at, slab(peer)], target.at[col, at, :], ssem.at[index, n],
-                 rsem.at[index, n], col=peer)
-            for n, peer in enumerate(col_peers)
-        ]
-
-    moved_e = [
-        send(energy.at[:, slab(peer)], ez.at[col], e_ssem.at[n], e_rsem.at[n], col=peer)
-        for n, peer in enumerate(col_peers)
-    ]
-    finish(pulls)
+        for peer in col_peers:
+            send(src.at[at, slab(peer)], target.at[col, at, :], ssem, rsem.at[index], col=peer)
+
+    others = pl.ds(0, cols - 1)
+
+    def piece_of(target, marks, index):
+        return target.at[others, pl.ds(marks[index], marks[index + 1] - marks[index]), :]
+
+    for peer in col_peers:
+        send(energy.at[:, slab(peer)], ez.at[col], e_sems.at[0], e_sems.at[1], col=peer)
+    for copy in pulls:
+        copy.wait()
 
     @pl.loop(0, cells // 16)
     def _(i):
@@ -305,8 +289,10 @@
         bound[at, :] = jnp.where(seeded, 1.0, jnp.where(irreversible[at, :] == 1, old, 0.0))
 
     order = (0, 4, 1, 2, 3)
-    moved_d = {n: move_piece(start, landing, n, d_ssem, d_rsem) for n in order}
-    moved_f = {n: move_piece(bound, fz, n, f_ssem, f_rsem) for n in order[:2]}
+    for n in order:
+        move_piece(start, landing, n, d_ssem.at[0], d_rsem)
+    for n in order[:2]:
+        move_piece(bound, fz, n, f_ssem.at[0], f_rsem)
     landing[col] = start[:, slab(col)]
     fz[col] = bound[:, slab(col)]
 
@@ -314,13 +300,14 @@
     sub = lax.broadcasted_iota(jnp.int32, (8, 128), 0)
     upper_half = sub < planes
     zero = jnp.zeros((8, 128), f32)
-    finish(fetch)
+    for copy in fetch:
+        copy.wait()
 
     def lane_of(a, n):
         return jnp.broadcast_to(a[:, n : n + 1], (8, 128))
 
     def corner_of(down, over, k):
-        tile = corner[2 * down + over, k]
+        tile = inverse[k, (cells - 8) * down : (cells - 8) * down + 8, (cells - 128) * over : (cells - 128) * over + 128]
         at = (7 if down else 0, 127 if over else 0)
         return jnp.broadcast_to(tile[at[0] : at[0] + 1, at[1] : at[1] + 1], (8, 128))
 
@@ -414,7 +401,7 @@
 
     upper_wide = lax.broadcasted_iota(jnp.int32, (8, cells), 0) < planes
     for j in range(x_blocks):
-        turned = gx[j].T
+        turned = inverse[col * x_blocks + j].T
         gx_high[j], gx_low[j] = split(turned)
         for side, at in ((0, 0), (1, last)):
             line = jnp.broadcast_to(turned[at : at + 1], (8, cells))
@@ -423,14 +410,29 @@
                 gend[side, x_blocks] = line
             else:
                 gend[side, x_blocks] = jnp.where(upper_wide, gend[side, x_blocks], line)
-    gy_both[:cells], gy_both[cells:] = split(gy[...])
+    gy = inverse[row]
+    gy_both[:cells], gy_both[cells:] = split(gy)
     gy_ends[0] = jnp.broadcast_to(gy[:, :1], (cells, 128))
     gy_ends[1] = jnp.broadcast_to(gy[:, last:], (cells, 128))
 
     for k in range(blocks):
         for side, at in ((0, 0), (1, 127)):
-            line = strips[side, k].T[at : at + 1]
+            strip = inverse[k, :, (cells - 128) * side : (cells - 128) * side + 128]
+            line = strip.T[at : at + 1]
             g_all[side, k] = jnp.broadcast_to(line, (8, cells))
+
+    @pl.when(above)
+    def _():
+        pl.semaphore_wait(greet.at[0], 1)
+
+    @pl.when(below)
+    def _():
+        signal_row(greet.at[0], row + 1)
+        pl.semaphore_wait(greet.at[1], 1)
+
+    @pl.when(above)
+    def _():
+        signal_row(greet.at[1], row - 1)
 
     first_col = jnp.where(col == 0, 1.0, 0.0)
     last_col = jnp.where(col == cols - 1, 1.0, 0.0)
@@ -462,12 +464,13 @@
                     dz[0, z, g, eight(i * 8 + 8), :] = tile[:, g * 128 : (g + 1) * 128]
 
     def share_rows(it):
-        return [
-            send(dz.at[it, :, :, pl.ds(cells, 8), :], dz.at[it, :, :, pl.ds(0, 8), :],
-                 v_ssem.at[it, 0], v_rsem.at[it, 0], row=lax.rem(row + 1, rows)),
-            send(dz.at[it, :, :, pl.ds(8, 8), :], dz.at[it, :, :, pl.ds(cells + 8, 8), :],
-                 v_ssem.at[it, 1], v_rsem.at[it, 1], row=lax.rem(row + rows - 1, rows)),
-        ]
+        send(dz.at[it, :, :, pl.ds(cells, 8), :], dz.at[it, :, :, pl.ds(0, 8), :],
+             v_sems.at[0, it], v_sems.at[1, it], row=lax.rem(row + 1, rows))
+        send(dz.at[it, :, :, pl.ds(8, 8), :], dz.at[it, :, :, pl.ds(cells + 8, 8), :],
+             v_sems.at[0, it], v_sems.at[1, it], row=lax.rem(row + rows - 1, rows))
+
+    def two_rows(it):
+        return dz.at[it, :, :, pl.ds(0, 16), :]
 
     def mirror(it):
         for z in range(planes):
@@ -596,10 +599,8 @@
             total = term if total is None else total + term
         x_send[it] = total
         x_all[it, col] = total
-        return [
-            send(x_send.at[it], x_all.at[it, col], x_ssem.at[it, n], x_rsem.at[it, n], col=peer)
-            for n, peer in enumerate(col_peers)
-        ]
+        for peer in col_peers:
+            send(x_send.at[it], x_all.at[it, col], x_sems.at[0, it], x_sems.at[1, it], col=peer)
 
     def y_share(it):
         sides = []
@@ -628,11 +629,9 @@
         y_send[it, 0] = lines[1]
         y_send[it, 1] = lines[0] + wide(wy_turn[...]) * lines[1]
         y_all[it, row] = lines[1]
-        sent = [
-            send(y_send.at[it, lax.div(row + n + 1, rows)], y_all.at[it, row], y_ssem.at[it, n],
-                 y_rsem.at[it, n], row=peer)
-            for n, peer in enumerate(row_peers)
-        ]
+        for n, peer in enumerate(row_peers):
+            send(y_send.at[it, lax.div(row + n + 1, rows)], y_all.at[it, row], y_sems.at[0, it],
+                 y_sems.at[1, it], row=peer)
         stacked = jnp.concatenate(sides + [jnp.zeros((112, cells), f32)], axis=0).T
         for t in range(cells // 8):
             here = slice(t * 8, t * 8 + 8)
@@ -646,7 +645,7 @@
                         + tile[:, n : n + 1] * gend[0, j]
                         + tile[:, 8 + n : 9 + n] * gend[1, j]
                     )
-        finish(sent)
+        finish(y_sems.at[1, it], y_all.at[it, pl.ds(0, rows - 1)])
         carried = []
         for side in range(2):
             total = wide(wy_in[side, 0]) * y_all[it, 0]
@@ -682,35 +681,37 @@
     def stream(it, ready):
         ready(order[0])
         ready(order[1])
-        shared = share_rows(it)
-        finish(shared)
-        mirror(it)
-        ranges = [(0, cuts[1] - 16), (cuts[4] + 16, cells)]
-        for a, b in ranges:
-            residual(it, a, b)
-        x_product(it, ranges)
+        share_rows(it)
+        a = 16
         for n in order[2:]:
             ready(n)
-            a, b = cuts[n] - 16, cuts[n + 1] - 16
+            b = cuts[n + 1] - 16
             if n == order[-1]:
                 b += 32
             residual(it, a, b)
             x_product(it, [(a, b)])
-        x_ends()
+            a = b
+            if n == order[2]:
+                finish(v_sems.at[1, it], two_rows(it))
+                mirror(it)
+                residual(it, 0, 16)
+                residual(it, cuts[4] + 16, cells)
+                x_product(it, [(0, 16), (cuts[4] + 16, cells)])
 
     def arrived(n):
-        finish(moved_d[n])
+        finish(d_rsem.at[n], piece_of(landing, cuts, n))
         regroup(cuts[n], cuts[n + 1])
 
-    finish(moved_e)
+    finish(e_sems.at[1], ez.at[others])
     scale_energy()
     stream(0, arrived)
-    sent = x_share(0)
+    x_ends()
+    x_share(0)
     for n in order[2:]:
-        moved_f[n] = move_piece(bound, fz, n, f_ssem, f_rsem)
+        move_piece(bound, fz, n, f_ssem.at[0], f_rsem)
     for z in range(planes):
         y_product(0, z)
-    finish(sent)
+    finish(x_sems.at[1, 0], x_all.at[0, others])
     y_share(0)
 
     totals = []
@@ -718,20 +719,18 @@
     held = [blank]
 
     def settled(n):
-        finish(moved_f[n])
+        finish(f_rsem.at[n], piece_of(fz, cuts, n))
         held.append(settle(0, cuts[n], cuts[n + 1], held.pop()))
 
     stream(1, settled)
     def give_back(n, m):
         at = pl.ds(backs_at[n], backs_at[n + 1] - backs_at[n])
-        return send(final.at[col_peers[m], at, :], out.at[at, slab(col)], back_ssem.at[n, m],
-                    back_rsem.at[n, m], col=col_peers[m])
-
-    backs = [[] for _ in backs_at[1:]]
+        send(final.at[col_peers[m], at, :], out.at[at, slab(col)], back_ssem.at[0],
+             back_rsem.at[n], col=col_peers[m])
 
     def give_all(n):
         for m in range(cols - 1):
-            backs[n].append(give_back(n, m))
+            give_back(n, m)
 
     def complete(low, high):
         @pl.loop(low // 8, high // 8)
@@ -752,14 +751,15 @@
                 )
                 out[here, block] = jnp.minimum(jnp.maximum(value, bound[here, block]), 1.0)
 
-    sent = x_share(1)
     for m in range(cols - 1):
         y_product(1, col_peers[m])
-        for n in range(2):
-            backs[n].append(give_back(n, m))
+        give_back(0, m)
+    x_ends()
+    x_share(1)
+    give_all(1)
     y_product(1, col)
     out[:, slab(col)] = final[col]
-    finish(sent)
+    finish(x_sems.at[1, 1], x_all.at[1, others])
     sides, carried = y_share(1)
     for z in range(planes):
         for j in range(x_blocks):
@@ -769,31 +769,25 @@
                 word_send[z, at : at + 1, :] = STEP * sides[side][n : n + 1]
                 at += 2 * x_blocks
                 word_send[z, at : at + 1, :] = STEP * carried[side][n : n + 1]
-    words = [
-        send(word_send.at[peer], word_all.at[col], w_ssem.at[n], w_rsem.at[n], col=peer)
-        for n, peer in enumerate(col_peers)
-    ]
+    for peer in col_peers:
+        send(word_send.at[peer], word_all.at[col], w_sems.at[0], w_sems.at[1], col=peer)
     give_all(2)
     word_all[col] = word_send[col]
     totals.append(jnp.sum(held[0]))
     totals.append(jnp.sum(settle(ITERS - 1, 0, cells, blank)))
     s_send[...] = jnp.where(sub == 0, totals[0], jnp.where(sub == 1, totals[1], 0.0))
-    shares = [
-        send(s_send, s_row.at[n], sr_ssem.at[n], sr_rsem.at[n], row=peer)
-        for n, peer in enumerate(row_peers)
-    ]
-    finish(shares)
+    for n, peer in enumerate(row_peers):
+        send(s_send, s_row.at[n], s_sems.at[0], s_sems.at[1], row=peer)
+    finish(s_sems.at[1], s_row)
     total = s_send[...]
     for n in range(rows - 1):
         total = total + s_row[n]
     s_col_send[...] = total
-    shares = [
-        send(s_col_send, s_col.at[n], sc_ssem.at[n], sc_rsem.at[n], col=peer)
-        for n, peer in enumerate(col_peers)
-    ]
+    for n, peer in enumerate(col_peers):
+        send(s_col_send, s_col.at[n], s_sems.at[2], s_sems.at[3], col=peer)
     for n in range(3, len(backs_at) - 1):
         give_all(n)
-    finish(words)
+    finish(w_sems.at[1], word_all.at[others])
     x_cols[...] = jnp.concatenate(
         [word_all[c] for c in range(cols)] + [jnp.zeros((128 - 8 * cols, cells), f32)], axis=0
     ).T
@@ -804,15 +798,27 @@
                 word_all[k // x_blocks, at : at + 1, :], (8, cells)
             )
     for n in range(len(backs_at) - 2):
-        finish(backs[n])
+        finish(back_rsem.at[n], piece_of(final, backs_at, n))
         complete(backs_at[n], backs_at[n + 1])
-    finish(shares)
+    finish(s_sems.at[3], s_col)
     for n in range(cols - 1):
         total = total + s_col[n]
     sizes = jnp.sqrt(total / cell_count + EPSILON) / STEP
     norms[...] = jnp.where(lane == 0, sizes[:1, :], sizes[1:2, :])[0, :ITERS]
-    finish(backs[-1])
-    complete(backs_at[-2], backs_at[-1])
+    for it in range(ITERS):
+        finish(x_sems.at[0, it], x_all.at[it, others])
+        finish(y_sems.at[0, it], y_all.at[it, pl.ds(0, rows - 1)])
+        finish(v_sems.at[0, it], two_rows(it))
+    finish(e_sems.at[0], ez.at[others])
+    finish(d_ssem.at[0], landing.at[others])
+    finish(f_ssem.at[0], fz.at[others])
+    finish(w_sems.at[0], word_all.at[others])
+    finish(s_sems.at[0], s_row)
+    finish(s_sems.at[2], s_col)
+    n = len(backs_at) - 2
+    finish(back_rsem.at[n], piece_of(final, backs_at, n))
+    complete(backs_at[n], backs_at[n + 1])
+    finish(back_ssem.at[0], final.at[others])
 
 
 def local(energy, damage_old, crack_seeds, irreversible, line_inverses, z_inverse):
@@ -824,7 +830,7 @@
     kinds = 2 * x_blocks + 2
     step = cells // 16
     cuts = (0, 3 * step, 8 * step, 12 * step, 13 * step, cells)
-    backs_at = (0, 4 * step, 8 * step, 11 * step, 14 * step, cells)
+    backs_at = (0, 2 * step, 8 * step, 12 * step, 15 * step, cells)
     cell_count = float(cols * rows * cells * line_length)
     shape = (rows, cols, cells, width, x_blocks, blocks, cell_count, cuts, backs_at)
     f32 = jnp.float32
@@ -856,9 +862,7 @@
             pltpu.VMEM((cols, cells, width), bf16),
             pltpu.VMEM((cols, cells, width), bf16),
             pltpu.VMEM((cols, cells, width), f32),
-            pltpu.VMEM((4, blocks, 8, 128), f32),
-            pltpu.VMEM((x_blocks, cells, cells), f32),
-            pltpu.VMEM((cells, cells), f32),
+            pltpu.VMEM((blocks, cells, cells), f32),
             pltpu.VMEM((x_blocks, cells, cells), bf16),
             pltpu.VMEM((x_blocks, cells, cells), bf16),
             pltpu.VMEM((2 * cells, cells), bf16),
@@ -874,7 +878,6 @@
             pltpu.VMEM((cells, 128), f32),
             pltpu.VMEM((cols, 8, 128), f32),
             pltpu.VMEM((2, cols, 8, cells), f32),
-            pltpu.VMEM((2, blocks, cells, 128), f32),
             pltpu.VMEM((2, blocks, 8, cells), f32),
             pltpu.VMEM((cols, 8, cells), f32),
             pltpu.VMEM((cols, 8, cells), f32),
@@ -889,27 +892,20 @@
             pltpu.VMEM((8, 128), f32),
             pltpu.VMEM((cols - 1, 8, 128), f32),
             pltpu.SMEM((cols, cols), f32),
-            dma((x_blocks + 12,)),
-            dma((cols - 1,)),
-            dma((cols - 1,)),
-            dma((5, cols - 1)),
-            dma((5, cols - 1)),
-            dma((5, cols - 1)),
-            dma((5, cols - 1)),
-            dma((5, cols - 1)),
-            dma((5, cols - 1)),
-            dma((cols - 1,)),
-            dma((cols - 1,)),
-            dma((ITERS, cols - 1)),
-            dma((ITERS, cols - 1)),
-            dma((ITERS, 2)),
-            dma((ITERS, 2)),
-            dma((ITERS, rows - 1)),
-            dma((ITERS, rows - 1)),
-            dma((cols - 1,)),
-            dma((cols - 1,)),
-            dma((rows - 1,)),
-            dma((rows - 1,)),
+            dma((6,)),
+            pltpu.SemaphoreType.REGULAR((2,)),
+            dma((2,)),
+            dma((1,)),
+            dma((5,)),
+            dma((1,)),
+            dma((5,)),
+            dma((1,)),
+            dma((5,)),
+            dma((2,)),
+            dma((2, ITERS)),
+            dma((2, ITERS)),
+            dma((2, ITERS)),
+            dma((4,)),
         ],
         compiler_params=pltpu.CompilerParams(
             has_side_effects=True, collective_id=0, vmem_limit_bytes=60 * 1024 * 1024

time: 108 us -> 105 us (0.972)
  Pallas kernels: 105 us -> 102 us
    pallas_call x1, Pallas kernels: 105 us -> 102 us  [local(): pl.pallas_call(functools.partial(line_kernel, shape), out_shape=(pltpu.VM...]
where the time goes in v5:
time: 105 us; the launch traced here: 104 us
  Pallas kernels  102 us (97%)
  local copies, waits for them, and re-layouts  1.83 us (2%)
    pallas_call x1, Pallas kernels, local(): pl.pallas_call(functools.partial(line_kernel, shape), out_shape=(pltpu.VM...  102 us

profile of v5, /device:TPU:0, one launch (start us, length us, event | category | flops | bytes accessed | tf_op | source)
XLA Modules:
  0.0 104.4 jit_solution(5520420703395911301)
XLA Ops:
  0.6 101.9 %line_iterations.1 = (f32[256,2048]{1,0:T(8,128)S(1)}, f32[2]{0:T(128)S(1)}) custom-call(f32[4,4]{1,0:T(4,128)} %z_hbm.1, f32[256,2048]{1,0:T(8,128)} %bitcast.6, f32[256,2048]{1,0:T(8,128)} %bitcast.7, s32[256,2048]{1,0:T(8,128)} %bitcast.8, s32[256,2048]{1,0:T(8,128)} %bitcast.9, f32[8,256,256]{2,1,0:T(8,128)} %inverses.1), custom_call_target="tpu_custom_call" | custom-call | tf_op jit(solution)/shard_map/line_iterations/pallas_call | solution.py:840
  102.5 1.3 %copy.10 = f32[1,256,2048]{2,1,0:T(8,128)} copy(f32[1,256,2048]{2,1,0:T(8,128)S(1)} %bitcast.5) | data formatting | bytes 4194304
  103.9 0.5 copy.11

commit v6 on v5

--- a/solution.py
+++ b/solution.py
@@ -164,7 +164,6 @@
     wy_turn,
     carry_rows,
     own_rows,
-    packed,
     w_mix,
     y_base,
     g_all,
@@ -516,15 +515,7 @@
                         total = total + mixing[z][k] * value[k]
                     w_high[z, here, lanes], w_low[z, here, lanes] = split(total)
 
-    def x_product(it, ranges):
-        packs = [jnp.zeros((b - a, 128), f32) for a, b in ranges]
-        spots = [lax.broadcasted_iota(jnp.int32, (b - a, 128), 1) for a, b in ranges]
-
-        def place(n, tile, lane_from, lane_to):
-            if lane_from != lane_to:
-                tile = pltpu.roll(tile, (lane_to - lane_from) % 128, 1)
-            packs[n] = jnp.where(spots[n] == lane_to, tile, packs[n])
-
+    def x_product(ranges):
         for j in range(x_blocks):
             block = slice(j * cells, (j + 1) * cells)
             parts = [(z, n) for z in range(planes) for n in range(len(ranges))]
@@ -543,14 +534,6 @@
                 part = along[at : at + c.stop - c.start]
                 at += c.stop - c.start
                 a_high[z, c, block], a_low[z, c, block] = split(part)
-                place(n, part[:, :128], 0, j * planes + z)
-                place(n, part[:, cells - 128 :], 127, (x_blocks + j) * planes + z)
-        for n, (a, b) in enumerate(ranges):
-            for z in range(planes):
-                near = pl.ds(8 + a, b - a)
-                place(n, dz[it, z, 0, near, :], 0, 2 * x_blocks * planes + z)
-                place(n, dz[it, z, groups - 1, near, :], 127, (2 * x_blocks + 1) * planes + z)
-            packed[a:b, :] = packs[n]
 
     def y_times(high, low):
         twice = dot(gy_both[...], high)
@@ -563,11 +546,39 @@
             for j in range(x_blocks):
                 y_base[side, z, j : j + 1, :] = both[at : at + 1, j * cells : (j + 1) * cells]
         if it + 1 == ITERS:
-            d = jnp.concatenate([dz[it, z, g, pl.ds(8, cells), :] for g in range(groups)], axis=1)
-            final[z] = d + STEP * both
-
-    def x_ends():
-        turned = y_times(*split(packed[...])).T
+            low = backs_at[1]
+            rest = pl.ds(8 + low, cells - low)
+            d = jnp.concatenate([dz[it, z, g, rest, :] for g in range(groups)], axis=1)
+            final[z, low:, :] = d + STEP * both[low:]
+
+    def y_first(it, z):
+        count = backs_at[1]
+        pair = jnp.concatenate([gy_both[:count], gy_both[cells : cells + count]], axis=0)
+        twice = dot(pair, a_high[z])
+        both = twice[:count] + (twice[count:] + dot(gy_both[:count], a_low[z]))
+        d = jnp.concatenate([dz[it, z, g, pl.ds(8, count), :] for g in range(groups)], axis=1)
+        final[z, :count, :] = d + STEP * both
+
+    def x_ends(it):
+        tile_lane = lax.broadcasted_iota(jnp.int32, (cells, 128), 1)
+        near = pl.ds(8, cells)
+        pack = jnp.zeros((cells, 128), f32)
+        for z in range(planes):
+            tiles = []
+            for j in range(x_blocks):
+                for spot, at, start_lane in (
+                    (j, j * cells, 0), (x_blocks + j, (j + 1) * cells - 128, 127)
+                ):
+                    lanes = slice(at, at + 128)
+                    tile = a_high[z, :, lanes].astype(f32) + a_low[z, :, lanes].astype(f32)
+                    tiles.append((tile, start_lane, spot * planes + z))
+            tiles.append((dz[it, z, 0, near, :], 0, 2 * x_blocks * planes + z))
+            tiles.append((dz[it, z, groups - 1, near, :], 127, (2 * x_blocks + 1) * planes + z))
+            for tile, lane_from, lane_to in tiles:
+                if lane_from != lane_to:
+                    tile = pltpu.roll(tile, (lane_to - lane_from) % 128, 1)
+                pack = jnp.where(tile_lane == lane_to, tile, pack)
+        turned = y_times(*split(pack)).T
 
         def keep(n, tile):
             other = pltpu.roll(tile, planes, 0)
@@ -685,18 +696,16 @@
         a = 16
         for n in order[2:]:
             ready(n)
-            b = cuts[n + 1] - 16
-            if n == order[-1]:
-                b += 32
+            b = cuts[n + 1] - 16 if n != order[-1] else cuts[4] + 16
             residual(it, a, b)
-            x_product(it, [(a, b)])
+            x_product([(a, b)])
             a = b
             if n == order[2]:
                 finish(v_sems.at[1, it], two_rows(it))
                 mirror(it)
                 residual(it, 0, 16)
                 residual(it, cuts[4] + 16, cells)
-                x_product(it, [(0, 16), (cuts[4] + 16, cells)])
+                x_product([(0, 16), (cuts[4] + 16, cells)])
 
     def arrived(n):
         finish(d_rsem.at[n], piece_of(landing, cuts, n))
@@ -705,7 +714,7 @@
     finish(e_sems.at[1], ez.at[others])
     scale_energy()
     stream(0, arrived)
-    x_ends()
+    x_ends(0)
     x_share(0)
     for n in order[2:]:
         move_piece(bound, fz, n, f_ssem.at[0], f_rsem)
@@ -752,11 +761,14 @@
                 out[here, block] = jnp.minimum(jnp.maximum(value, bound[here, block]), 1.0)
 
     for m in range(cols - 1):
+        y_first(1, col_peers[m])
+        give_back(0, m)
+    x_ends(1)
+    x_share(1)
+    for m in range(cols - 1):
         y_product(1, col_peers[m])
-        give_back(0, m)
-    x_ends()
-    x_share(1)
-    give_all(1)
+        give_back(1, m)
+    y_first(1, col)
     y_product(1, col)
     out[:, slab(col)] = final[col]
     finish(x_sems.at[1, 1], x_all.at[1, others])
@@ -821,6 +833,19 @@
     finish(back_ssem.at[0], final.at[others])
 
 
+def hand_over(damage, norms, damage_out, norms_out, sems):
+    parts = 4
+    part = damage.shape[0] // parts
+    copies = [pltpu.make_async_copy(norms, norms_out, sems.at[parts])]
+    for n in range(parts):
+        at = pl.ds(n * part, part)
+        copies.append(pltpu.make_async_copy(damage.at[at], damage_out.at[0, at], sems.at[n]))
+    for copy in copies:
+        copy.start()
+    for copy in copies:
+        copy.wait()
+
+
 def local(energy, damage_old, crack_seeds, irreversible, line_inverses, z_inverse):
     planes, cells, line_length = energy.shape
     rows, cols = lax.axis_size("row"), lax.axis_size("col")
@@ -830,7 +855,7 @@
     kinds = 2 * x_blocks + 2
     step = cells // 16
     cuts = (0, 3 * step, 8 * step, 12 * step, 13 * step, cells)
-    backs_at = (0, 2 * step, 8 * step, 12 * step, 15 * step, cells)
+    backs_at = (0, 2 * step, 10 * step, 13 * step, 15 * step, cells)
     cell_count = float(cols * rows * cells * line_length)
     shape = (rows, cols, cells, width, x_blocks, blocks, cell_count, cuts, backs_at)
     f32 = jnp.float32
@@ -875,7 +900,6 @@
             pltpu.VMEM((8, 128), f32),
             pltpu.VMEM((2 * cols, 8, width), f32),
             pltpu.VMEM((kinds, 8, cells), f32),
-            pltpu.VMEM((cells, 128), f32),
             pltpu.VMEM((cols, 8, 128), f32),
             pltpu.VMEM((2, cols, 8, cells), f32),
             pltpu.VMEM((2, blocks, 8, cells), f32),
@@ -919,7 +943,21 @@
         irreversible[0],
         line_inverses,
     )
-    return damage[None], norms
+    return pl.pallas_call(
+        hand_over,
+        out_shape=(
+            jax.ShapeDtypeStruct((1, cells, line_length), f32),
+            jax.ShapeDtypeStruct((ITERS,), f32),
+        ),
+        in_specs=[vmem, vmem],
+        out_specs=(pl.BlockSpec(memory_space=pl.ANY), pl.BlockSpec(memory_space=pl.ANY)),
+        scratch_shapes=[dma((5,))],
+        compiler_params=pltpu.CompilerParams(vmem_limit_bytes=1024 * 1024),
+        name="hand_over",
+    )(
+        pltpu.with_memory_space_constraint(damage, pltpu.VMEM),
+        pltpu.with_memory_space_constraint(norms, pltpu.VMEM),
+    )
 
 
 def solution(mesh):

time: 105 us -> 103 us (0.981)
  local copies, waits for them, and re-layouts: 1.83 us -> 0 us
    unnamed x2 -> x0, local copies, waits for them, and re-layouts: 1.83 us -> none
    pallas_call x0 -> x1, Pallas kernels: none -> 1.36 us  [local(): pl.pallas_call(hand_over, out_shape=(jax.ShapeDtypeStruct((1, cells, line...]
where the time goes in v6:
time: 103 us
  Pallas kernels  103 us (100%)
    pallas_call x1, Pallas kernels, local(): pl.pallas_call(functools.partial(line_kernel, shape), out_shape=(pltpu.VM...  101 us

profile of v6, /device:TPU:0, one launch (start us, length us, event | category | flops | bytes accessed | tf_op | source)
XLA Modules:
  0.0 103.3 jit_solution(14223010607160341143)
XLA Ops:
  0.6 101.3 %line_iterations.1 = (f32[256,2048]{1,0:T(8,128)S(1)}, f32[2]{0:T(128)S(1)}) custom-call(f32[4,4]{1,0:T(4,128)} %z_hbm.1, f32[256,2048]{1,0:T(8,128)} %bitcast.4, f32[256,2048]{1,0:T(8,128)} %bitcast.5, s32[256,2048]{1,0:T(8,128)} %bitcast.6, s32[256,2048]{1,0:T(8,128)} %bitcast.7, f32[8,256,256]{2,1,0:T(8,128)} %inverses.1), custom_call_target="tpu_custom_call" | custom-call | tf_op jit(solution)/shard_map/line_iterations/pallas_call | solution.py:865
  101.9 1.4 %hand_over.1 = (f32[1,256,2048]{2,1,0:T(8,128)}, f32[2]{0:T(128)}) custom-call(f32[256,2048]{1,0:T(8,128)S(1)} %get-tuple-element.4.damage, f32[2]{0:T(128)S(1)} %get-tuple-element.5.norms), custom_call_target="tpu_custom_call" | custom-call | tf_op jit(solution)/shard_map/hand_over/pallas_call | solution.py:946

commit v7 on v6

--- a/solution.py
+++ b/solution.py
@@ -138,12 +138,14 @@
     damage_old,
     crack_seeds,
     irreversible,
+    e_home,
     start,
     bound,
     ez,
     ec,
     fz,
     landing,
+    dx,
     dz,
     final,
     w_high,
@@ -255,11 +257,16 @@
         pltpu.make_async_copy(irreversible_hbm, irreversible, local_sems.at[2]),
     ]
     fetch = [
-        pltpu.make_async_copy(energy.at[:, slab(col)], ez.at[col], local_sems.at[3]),
         pltpu.make_async_copy(inverses, inverse, local_sems.at[4]),
         pltpu.make_async_copy(z_hbm, z_inv, local_sems.at[5]),
     ]
-    for copy in pulls + fetch:
+    e_cuts = (0, cells // 8, cells)
+    e_parts = [pl.ds(a, b - a) for a, b in zip(e_cuts, e_cuts[1:])]
+    loads = [
+        pltpu.make_async_copy(energy.at[at], e_home.at[at], local_sems.at[(3, 6)[n]])
+        for n, at in enumerate(e_parts)
+    ]
+    for copy in loads + pulls + fetch:
         copy.start()
     neighbours = jnp.where(above, 1, 0) + jnp.where(below, 1, 0)
     pl.semaphore_wait(barrier, cols - 1 + neighbours)
@@ -274,8 +281,10 @@
     def piece_of(target, marks, index):
         return target.at[others, pl.ds(marks[index], marks[index + 1] - marks[index]), :]
 
-    for peer in col_peers:
-        send(energy.at[:, slab(peer)], ez.at[col], e_sems.at[0], e_sems.at[1], col=peer)
+    for copy, at in zip(loads, e_parts):
+        copy.wait()
+        for peer in col_peers:
+            send(e_home.at[at, slab(peer)], ez.at[col, at, :], e_sems.at[0], e_sems.at[1], col=peer)
     for copy in pulls:
         copy.wait()
 
@@ -292,6 +301,7 @@
         move_piece(start, landing, n, d_ssem.at[0], d_rsem)
     for n in order[:2]:
         move_piece(bound, fz, n, f_ssem.at[0], f_rsem)
+    ez[col] = e_home[:, slab(col)]
     landing[col] = start[:, slab(col)]
     fz[col] = bound[:, slab(col)]
 
@@ -435,8 +445,19 @@
 
     first_col = jnp.where(col == 0, 1.0, 0.0)
     last_col = jnp.where(col == cols - 1, 1.0, 0.0)
-    lane16 = lax.broadcasted_iota(jnp.int32, (16, 128), 1)
-    at_first, at_last = lane16 == 0, lane16 == 127
+    at_first, at_last = lane == 0, lane == 127
+
+    def keep_damage(it, z, at, row_of):
+        tiles = [row_of[:, g * 128 : (g + 1) * 128] for g in range(groups)]
+        up = [pltpu.roll(tile, 1, 1) for tile in tiles]
+        down = [pltpu.roll(tile, 127, 1) for tile in tiles]
+        for g in range(groups):
+            before = up[g - 1] if g > 0 else tiles[g] * first_col
+            after = down[g + 1] if g < groups - 1 else tiles[g] * last_col
+            dz[it, z, g, eight(at + 8), :] = tiles[g]
+            dx[z, eight(at), g * 128 : (g + 1) * 128] = jnp.where(
+                at_first, before, up[g]
+            ) + jnp.where(at_last, after, down[g])
 
     mixing = [[KAPPA * z_inv[z, k] for k in range(planes)] for z in range(planes)]
     for k in range(planes):
@@ -458,9 +479,7 @@
         @pl.loop(low // 8, high // 8)
         def _(i):
             for z in range(planes):
-                tile = landing[z, eight(i * 8), :]
-                for g in range(groups):
-                    dz[0, z, g, eight(i * 8 + 8), :] = tile[:, g * 128 : (g + 1) * 128]
+                keep_damage(0, z, i * 8, landing[z, eight(i * 8), :])
 
     def share_rows(it):
         send(dz.at[it, :, :, pl.ds(cells, 8), :], dz.at[it, :, :, pl.ds(0, 8), :],
@@ -496,14 +515,7 @@
                 for z in range(planes):
                     d = mids[z]
                     near = dz[it, z, g, pl.ds(base + 7, 16), :] + dz[it, z, g, pl.ds(base + 9, 16), :]
-                    before = d * first_col
-                    if g > 0:
-                        before = pltpu.roll(dz[it, z, g - 1, padded, :], 1, 1)
-                    after = d * last_col
-                    if g < groups - 1:
-                        after = pltpu.roll(dz[it, z, g + 1, padded, :], 127, 1)
-                    near = near + jnp.where(at_first, before, pltpu.roll(d, 1, 1))
-                    near = near + jnp.where(at_last, after, pltpu.roll(d, 127, 1))
+                    near = near + dx[z, here, lanes]
                     if z > 0:
                         near = near + mids[z - 1]
                     if z < planes - 1:
@@ -681,8 +693,7 @@
                 d = jnp.concatenate([dz[it, z, g, padded, :] for g in range(groups)], axis=1)
                 renewed = jnp.minimum(jnp.maximum(d + STEP * solved, fz[z, here, :]), 1.0)
                 if it + 1 < ITERS:
-                    for g in range(groups):
-                        dz[it + 1, z, g, padded, :] = renewed[:, g * 128 : (g + 1) * 128]
+                    keep_damage(it + 1, z, i * 8, renewed)
                 change = renewed - d
                 acc = acc + change * change
             return acc
@@ -876,6 +887,8 @@
             pltpu.VMEM((cells, line_length), jnp.int32),
             pltpu.VMEM((cells, line_length), f32),
             pltpu.VMEM((cells, line_length), f32),
+            pltpu.VMEM((cells, line_length), f32),
+            pltpu.VMEM((cols, cells, width), f32),
             pltpu.VMEM((cols, cells, width), f32),
             pltpu.VMEM((cols, cells, width), f32),
             pltpu.VMEM((cols, cells, width), f32),
@@ -916,7 +929,7 @@
             pltpu.VMEM((8, 128), f32),
             pltpu.VMEM((cols - 1, 8, 128), f32),
             pltpu.SMEM((cols, cols), f32),
-            dma((6,)),
+            dma((7,)),
             pltpu.SemaphoreType.REGULAR((2,)),
             dma((2,)),
             dma((1,)),

time: 103 us -> 103 us (level)
  no operation moved by 1% of the time
where the time goes in v7:
time: 103 us
  Pallas kernels  103 us (100%)
    pallas_call x1, Pallas kernels, local(): pl.pallas_call(functools.partial(line_kernel, shape), out_shape=(pltpu.VM...  101 us

profile of v7, /device:TPU:0, one launch (start us, length us, event | category | flops | bytes accessed | tf_op | source)
XLA Modules:
  0.0 103.2 jit_solution(17824004483324321646)
XLA Ops:
  0.6 101.2 %line_iterations.1 = (f32[256,2048]{1,0:T(8,128)S(1)}, f32[2]{0:T(128)S(1)}) custom-call(f32[4,4]{1,0:T(4,128)} %z_hbm.1, f32[256,2048]{1,0:T(8,128)} %bitcast.4, f32[256,2048]{1,0:T(8,128)} %bitcast.5, s32[256,2048]{1,0:T(8,128)} %bitcast.6, s32[256,2048]{1,0:T(8,128)} %bitcast.7, f32[8,256,256]{2,1,0:T(8,128)} %inverses.1), custom_call_target="tpu_custom_call" | custom-call | tf_op jit(solution)/shard_map/line_iterations/pallas_call | solution.py:876
  101.8 1.4 %hand_over.1 = (f32[1,256,2048]{2,1,0:T(8,128)}, f32[2]{0:T(128)}) custom-call(f32[256,2048]{1,0:T(8,128)S(1)} %get-tuple-element.4.damage, f32[2]{0:T(128)S(1)} %get-tuple-element.5.norms), custom_call_target="tpu_custom_call" | custom-call | tf_op jit(solution)/shard_map/hand_over/pallas_call | solution.py:959

commit v8 on v7

--- a/solution.py
+++ b/solution.py
@@ -476,7 +476,7 @@
                 ec[z, eight(i * 8), :] = scaled + (1.0 / KAPPA + sides)
 
     def regroup(low, high):
-        @pl.loop(low // 8, high // 8)
+        @pl.loop(low // 8, high // 8, unroll=2)
         def _(i):
             for z in range(planes):
                 keep_damage(0, z, i * 8, landing[z, eight(i * 8), :])
@@ -698,7 +698,7 @@
                 acc = acc + change * change
             return acc
 
-        return lax.fori_loop(low // 8, high // 8, step, squares)
+        return lax.fori_loop(low // 8, high // 8, step, squares, unroll=2)
 
     def stream(it, ready):
         ready(order[0])

time: 103 us -> 103 us (level)
  no operation moved by 1% of the time
where the time goes in v8:
time: 103 us
  Pallas kernels  102 us (99%)
    pallas_call x1, Pallas kernels, local(): pl.pallas_call(functools.partial(line_kernel, shape), out_shape=(pltpu.VM...  101 us

profile of v8, /device:TPU:0, one launch (start us, length us, event | category | flops | bytes accessed | tf_op | source)
XLA Modules:
  0.0 102.8 jit_solution(7335469483526728654)
XLA Ops:
  0.6 100.8 %line_iterations.1 = (f32[256,2048]{1,0:T(8,128)S(1)}, f32[2]{0:T(128)S(1)}) custom-call(f32[4,4]{1,0:T(4,128)} %z_hbm.1, f32[256,2048]{1,0:T(8,128)} %bitcast.4, f32[256,2048]{1,0:T(8,128)} %bitcast.5, s32[256,2048]{1,0:T(8,128)} %bitcast.6, s32[256,2048]{1,0:T(8,128)} %bitcast.7, f32[8,256,256]{2,1,0:T(8,128)} %inverses.1), custom_call_target="tpu_custom_call" | custom-call | tf_op jit(solution)/shard_map/line_iterations/pallas_call | solution.py:876
  101.4 1.4 %hand_over.1 = (f32[1,256,2048]{2,1,0:T(8,128)}, f32[2]{0:T(128)}) custom-call(f32[256,2048]{1,0:T(8,128)S(1)} %get-tuple-element.4.damage, f32[2]{0:T(128)S(1)} %get-tuple-element.5.norms), custom_call_target="tpu_custom_call" | custom-call | tf_op jit(solution)/shard_map/hand_over/pallas_call | solution.py:959

commit v9 on v8

--- a/solution.py
+++ b/solution.py
@@ -753,7 +753,7 @@
             give_back(n, m)
 
     def complete(low, high):
-        @pl.loop(low // 8, high // 8)
+        @pl.loop(low // 8, high // 8, unroll=2)
         def _(i):
             here = eight(i * 8)
             tile = x_cols[here, :]

time: 103 us -> 103 us (level)
  no operation moved by 1% of the time
where the time goes in v9:
time: 103 us
  Pallas kernels  102 us (99%)
    pallas_call x1, Pallas kernels, local(): pl.pallas_call(functools.partial(line_kernel, shape), out_shape=(pltpu.VM...  101 us

profile of v9, /device:TPU:0, one launch (start us, length us, event | category | flops | bytes accessed | tf_op | source)
XLA Modules:
  0.0 102.7 jit_solution(13613023718787990380)
XLA Ops:
  0.6 100.7 %line_iterations.1 = (f32[256,2048]{1,0:T(8,128)S(1)}, f32[2]{0:T(128)S(1)}) custom-call(f32[4,4]{1,0:T(4,128)} %z_hbm.1, f32[256,2048]{1,0:T(8,128)} %bitcast.4, f32[256,2048]{1,0:T(8,128)} %bitcast.5, s32[256,2048]{1,0:T(8,128)} %bitcast.6, s32[256,2048]{1,0:T(8,128)} %bitcast.7, f32[8,256,256]{2,1,0:T(8,128)} %inverses.1), custom_call_target="tpu_custom_call" | custom-call | tf_op jit(solution)/shard_map/line_iterations/pallas_call | solution.py:876
  101.4 1.4 %hand_over.1 = (f32[1,256,2048]{2,1,0:T(8,128)}, f32[2]{0:T(128)}) custom-call(f32[256,2048]{1,0:T(8,128)S(1)} %get-tuple-element.4.damage, f32[2]{0:T(128)S(1)} %get-tuple-element.5.norms), custom_call_target="tpu_custom_call" | custom-call | tf_op jit(solution)/shard_map/hand_over/pallas_call | solution.py:959
